TPU v7x, 256 devices: a whole 4x4x8 slice. The times are simulated.
256 devices in a mesh: col: 32 (over z, y), row: 8 (over x, core).
Axes of the slice: x: 4, y: 4, z: 8, core: 2. Of those that a mesh axis runs over, the one named last changes fastest.
Arguments:
- w_gate: float32 [2048, 5120], P('row', 'col')
- w_up: float32 [2048, 5120], P('row', 'col')
- w_down: float32 [5120, 2048], P('row', 'col')
- x_norm: bfloat16 [16384, 2048], P(None, 'row')
- x_act: bfloat16 [16384, 5120], P(None, 'row')
- dy_gate: bfloat16 [16384, 5120], P(None, 'col')
- dy_up: bfloat16 [16384, 5120], P(None, 'col')
- dy_down: bfloat16 [16384, 2048], P(None, 'col')
- r_gate: float32 [2048], P('row')
- c_gate: float32 [5120], P('col')
- r_up: float32 [2048], P('row')
- c_up: float32 [5120], P('col')
- r_down: float32 [5120], P('row')
- c_down: float32 [2048], P('col')
- hyper_params: float32 [3], replicated
Outputs:
- output 1: float32 [2048, 5120], P('row', 'col')
- output 2: float32 [2048, 5120], P('row', 'col')
- output 3: float32 [5120, 2048], P('row', 'col')
- output 4: float32 [2048], P('row')
- output 5: float32 [5120], P('col')
- output 6: float32 [2048], P('row')
- output 7: float32 [5120], P('col')
- output 8: float32 [5120], P('row')
- output 9: float32 [2048], P('col')
- output 10: bfloat16 [16384, 2048], P(None, 'row')
- output 11: bfloat16 [16384, 5120], P(None, 'row')
All inputs are finite; a program needn't handle non-finite values.
Results may differ from a plain program's by a relative error of at most 0.001.
Values are sent between devices in bfloat16 or wider.
A program may use at most 768 MiB of HBM per device.

v0:
```python
import jax
import jax.numpy as jnp
from jax import lax
from jax.sharding import PartitionSpec as P

EPS_ONE = 1e-30
EPS_TWO = 1e-3


def factored_step(w_loc, grad_loc, r_loc, c_loc, hyper_params, m_total, n_total):
    beta_two = hyper_params[0]
    grad_sq = grad_loc * grad_loc + EPS_ONE
    row_sum = lax.psum(jnp.sum(grad_sq, axis=1), 'col')
    col_sum = lax.psum(jnp.sum(grad_sq, axis=0), 'row')
    r_new = beta_two * r_loc + (1.0 - beta_two) * (row_sum / n_total)
    c_new = beta_two * c_loc + (1.0 - beta_two) * (col_sum / m_total)
    r_mean = lax.psum(jnp.sum(r_new), 'row') / m_total
    update = grad_loc * lax.rsqrt(r_new[:, None] * c_new[None, :] / r_mean)
    u_sq = lax.psum(jnp.sum(update * update), ('row', 'col'))
    rms_u = jnp.sqrt(u_sq / (m_total * n_total))
    update_hat = update / jnp.maximum(1.0, rms_u / hyper_params[2])
    w_sq = lax.psum(jnp.sum(w_loc * w_loc), ('row', 'col'))
    step_size = hyper_params[1] * jnp.maximum(EPS_TWO, jnp.sqrt(w_sq / (m_total * n_total)))
    return w_loc - step_size * update_hat, r_new, c_new


def weight_grad(activations, grad_out):
    return lax.dot_general(activations, grad_out, (((0,), (0,)), ((), ())), preferred_element_type=jnp.float32)


def input_grad(grad_out, weight):
    return lax.dot_general(grad_out, weight.astype(jnp.bfloat16), (((1,), (1,)), ((), ())), preferred_element_type=jnp.float32)


def solution(mesh):
    row_size = mesh.shape['row']
    col_size = mesh.shape['col']
    weight_spec = P('row', 'col')
    act_spec = P(None, 'row')
    grad_spec = P(None, 'col')
    in_specs = (weight_spec,) * 3 + (act_spec, act_spec) + (grad_spec,) * 3 + (P('row'), P('col')) * 3 + (P(),)
    out_specs = (weight_spec,) * 3 + (P('row'), P('col')) * 3 + (act_spec, act_spec)

    def body(w_gate, w_up, w_down, x_norm, x_act, dy_gate, dy_up, dy_down, r_gate, c_gate, r_up, c_up, r_down, c_down, hyper_params):
        d_model = w_gate.shape[0] * row_size
        d_ff = w_gate.shape[1] * col_size
        new_gate, r_gate_new, c_gate_new = factored_step(w_gate, weight_grad(x_norm, dy_gate), r_gate, c_gate, hyper_params, d_model, d_ff)
        new_up, r_up_new, c_up_new = factored_step(w_up, weight_grad(x_norm, dy_up), r_up, c_up, hyper_params, d_model, d_ff)
        new_down, r_down_new, c_down_new = factored_step(w_down, weight_grad(x_act, dy_down), r_down, c_down, hyper_params, d_ff, d_model)
        dx_norm = lax.psum(input_grad(dy_gate, w_gate) + input_grad(dy_up, w_up), 'col').astype(jnp.bfloat16)
        dx_act = lax.psum(input_grad(dy_down, w_down), 'col').astype(jnp.bfloat16)
        return (new_gate, new_up, new_down, r_gate_new, c_gate_new, r_up_new, c_up_new, r_down_new, c_down_new, dx_norm, dx_act)

    return jax.shard_map(body, mesh=mesh, in_specs=in_specs, out_specs=out_specs, check_vma=False)
```

profile of v0, /device:TPU:1, one launch (start us, length us, event | category | flops | bytes accessed | tf_op | source)
XLA Modules:
  0.0 1440.7 jit_solution(18347725430569759927)
XLA Ops:
  0.6 0.0 copy-start
  0.7 0.0 copy-start.2
  0.7 0.0 copy-start.3
  0.7 1.6 copy-done
  2.2 9.6 fusion.4
  11.8 0.0 copy-done.2
  11.9 0.3 copy-done.3
  12.1 1.8 fusion.2
  13.9 0.7 copy-done.4
  14.6 1.6 fusion
  16.2 0.0 copy-done.7
  16.3 0.0 copy-start.6
  16.3 16.2 %fusion.6 = f32[16384,640]{1,0:T(8,128)} fusion(bf16[16384,64]{0,1:T(8,128)(2,1)S(1)} %copy-done, f32[640,64]{0,1:T(8,128)S(1)} %copy-done.7), kind=kOutput, calls=%fused_computation.22 | convolution fusion | flops 1342218240 | bytes 44204032 | tf_op jit(solution)/shard_map/dot_general | solution.py:32
  32.5 0.0 copy-done.6
  32.5 11.1 fusion.9
  43.6 0.0 copy-done.5
  43.6 14.2 convolution_add_fusion
  57.8 0.0 copy-start.20
  57.8 0.0 copy-start.16
  57.8 0.0 copy-start.17
  57.8 0.0 copy-start.1
  57.8 1271.2 %all-reduce.4 = (f32[256]{0:T(256)S(1)}, f32[256]{0:T(256)S(1)}, f32[640]{0:T(1024)S(1)}, bf16[16384,256]{1,0:T(8,128)(2,1)}, bf16[16384,640]{1,0:T(8,128)(2,1)}) all-reduce(f32[256]{0:T(256)S(1)} %get-tuple-element.16, f32[256]{0:T(256)S(1)} %get-tuple-element.14, ...), channel_id=1, replica_groups=mesh['col'=32,'row'=8] {'col'}, use_global_device_ids=true, to_apply=%region_3.0 | all-reduce | flops 14681216 | bytes 88089600 | tf_op jit(solution)/shard_map/psum | solution.py:13
  1329.0 0.0 copy-done.13
  1329.0 0.7 fusion.14
  1330.3 0.0 copy-done.18
  1330.3 0.0 copy-done.19
  1330.3 1.2 fusion.12
  1331.6 0.0 copy-done.15
  1331.6 1.2 fusion.11
  1332.8 16.8 %all-reduce.2 = (f32[]{:T(128)}, f32[160]{0:T(256)S(1)}, f32[]{:T(128)}, f32[160]{0:T(256)S(1)}, f32[]{:T(128)}, /*index=5*/f32[64]{0:T(128)S(1)}) all-reduce(f32[]{:T(128)} %get-tuple-element.46, f32[160]{0:T(256)S(1)} %get-tuple-element.15, f32[]{:T(128)} %get-tuple-element.36, ...), channel_id=1, replica_groups=mesh['col'=32,'row'=8] {'row'}, use_global_device_ids=true, to_apply=%region_7.0 | all-reduce | flops 387 | bytes 3096 | tf_op jit(solution)/shard_map/psum | solution.py:17
  1349.6 0.6 multiply_add_fusion.8
  1350.3 0.0 copy-start.14
  1350.9 0.7 multiply_reduce_fusion
  1351.7 0.0 copy-done.16
  1351.7 0.6 multiply_add_fusion.4
  1352.3 0.0 copy-start.9
  1352.9 0.7 multiply_reduce_fusion.2
  1353.6 0.0 copy-done.17
  1353.7 0.6 multiply_add_fusion.6
  1354.3 0.0 copy-start.10
  1355.0 0.7 multiply_reduce_fusion.4
  1355.7 0.6 multiply_reduce_fusion.3
  1356.3 0.6 multiply_reduce_fusion.1
  1357.0 73.1 %all-reduce = (f32[]{:T(128)}, f32[]{:T(128)}, f32[]{:T(128)}, f32[]{:T(128)}, f32[]{:T(128)}, /*index=5*/f32[]{:T(128)}) all-reduce(f32[]{:T(128)} %multiply_reduce_fusion.4, f32[]{:T(128)} %get-tuple-element.49, f32[]{:T(128)} %multiply_reduce_fusion.2, f32[]{:T(128)} %get-tuple-element.48, ...), channel_id=1, replica_groups=mesh['col'=32,'row'=8] {'row','col'}, use_global_device_ids=true, to_apply=%region_9.0 | all-reduce | flops 6 | bytes 48 | tf_op jit(solution)/shard_map/psum | solution.py:19
  1432.7 0.8 multiply_subtract_fusion
  1436.2 0.8 multiply_subtract_fusion.1
  1439.7 0.8 multiply_subtract_fusion.2
  1440.5 0.0 copy-done.12
  (17 shorter events, 0.0 us)
Async XLA Ops:
  0.6 1.6 copy-start
  0.7 11.2 copy-start.2
  0.7 11.5 copy-start.3
  12.1 2.5 copy-start.4
  14.6 1.6 copy-start.7
  16.3 16.2 %copy-start.6 = (f32[256,160]{0,1:T(8,128)S(1)}, f32[256,160]{0,1:T(8,128)}, u32[]{:S(2)}) copy-start(f32[256,160]{0,1:T(8,128)} %param.15) | copy-start | bytes 491524
  32.5 11.1 copy-start.5
  57.8 1271.2 %copy-start.13 = (f32[3]{0:T(128)S(1)}, f32[3]{0:T(128)}, u32[]{:S(2)}) copy-start(f32[3]{0:T(128)} %param.29) | copy-start | bytes 40
  57.8 1272.6 %copy-start.18 = (f32[256]{0:T(256)S(1)}, f32[256]{0:T(256)}, u32[]{:S(2)}) copy-start(f32[256]{0:T(256)} %param.25) | copy-start | bytes 3076
  57.8 1272.6 %copy-start.19 = (f32[256]{0:T(256)S(1)}, f32[256]{0:T(256)}, u32[]{:S(2)}) copy-start(f32[256]{0:T(256)} %param.23) | copy-start | bytes 3076
  57.8 1273.8 %copy-start.15 = (f32[640]{0:T(1024)S(1)}, f32[640]{0:T(1024)}, u32[]{:S(2)}) copy-start(f32[640]{0:T(1024)} %param.27) | copy-start | bytes 7684
  57.8 1291.8 %copy-start.20 = (f32[64]{0:T(128)S(1)}, f32[64]{0:T(128)}, u32[]{:S(2)}) copy-start(f32[64]{0:T(128)} %param.28) | copy-start | bytes 772
  57.8 1293.9 %copy-start.16 = (f32[160]{0:T(256)S(1)}, f32[160]{0:T(256)}, u32[]{:S(2)}) copy-start(f32[160]{0:T(256)} %param.26) | copy-start | bytes 1924
  57.8 1295.9 %copy-start.17 = (f32[160]{0:T(256)S(1)}, f32[160]{0:T(256)}, u32[]{:S(2)}) copy-start(f32[160]{0:T(256)} %param.24) | copy-start | bytes 1924
  57.8 1382.8 %copy-start.1 = (bf16[16384,64]{0,1:T(8,128)(2,1)S(1)}, bf16[16384,64]{0,1:T(8,128)(2,1)}, u32[]{:S(2)}) copy-start(bf16[16384,64]{0,1:T(8,128)(2,1)} %param.22) | copy-start | bytes 6291460
  1331.6 108.9 %copy-start.11 = (f32[256]{0:T(256)}, f32[256]{0:T(256)S(1)}, u32[]{:S(2)}) copy-start(f32[256]{0:T(256)S(1)} %get-tuple-element.37) | copy-start | bytes 3076
  1331.6 108.9 %copy-start.12 = (f32[256]{0:T(256)}, f32[256]{0:T(256)S(1)}, u32[]{:S(2)}) copy-start(f32[256]{0:T(256)S(1)} %get-tuple-element.47) | copy-start | bytes 3076
  1332.8 107.7 %copy-start.8 = (f32[640]{0:T(1024)}, f32[640]{0:T(1024)S(1)}, u32[]{:S(2)}) copy-start(f32[640]{0:T(1024)S(1)} %get-tuple-element.35) | copy-start | bytes 7684
  1350.3 90.3 %copy-start.14 = (f32[64]{0:T(128)}, f32[64]{0:T(128)S(1)}, u32[]{:S(2)}) copy-start(f32[64]{0:T(128)S(1)} %multiply_add_fusion.8) | copy-start | bytes 772
  1352.3 88.2 %copy-start.9 = (f32[160]{0:T(256)}, f32[160]{0:T(256)S(1)}, u32[]{:S(2)}) copy-start(f32[160]{0:T(256)S(1)} %multiply_add_fusion.4) | copy-start | bytes 1924
  1354.3 86.2 %copy-start.10 = (f32[160]{0:T(256)}, f32[160]{0:T(256)S(1)}, u32[]{:S(2)}) copy-start(f32[160]{0:T(256)S(1)} %multiply_add_fusion.6) | copy-start | bytes 1924
where the time goes:
time: 1440 us
  blocking collectives  1360 us (94%)
  matrix products  54.5 us (4%)
    psum x1, blocking collectives, factored_step(): row_sum = lax.psum(jnp.sum(grad_sq, axis=1), 'col')  1270 us
    psum x1, blocking collectives, factored_step(): u_sq = lax.psum(jnp.sum(update * update), ('row', 'col'))  73.1 us
    dot_general x3, matrix products, input_grad(): lax.dot_general(grad_out, weight.astype(jnp.bfloat16), (((1,), (1,)), (()...  41.5 us

commit v1 on v0

--- a/solution.py
+++ b/solution.py
@@ -1,10 +1,231 @@
 import jax
 import jax.numpy as jnp
 from jax import lax
+from jax.experimental import pallas as pl
+from jax.experimental.pallas import tpu as pltpu
 from jax.sharding import PartitionSpec as P
 
 EPS_ONE = 1e-30
 EPS_TWO = 1e-3
+MESH = pl.DeviceIdType.MESH
+NY, NZ, NX = 4, 8, 4
+NCOL, NROW = NY * NZ, NX * 2
+LONG = NCOL // 2
+BF16, F32 = jnp.bfloat16, jnp.float32
+
+
+def ring_place(cycle, col):
+    y, z = col % NY, col // NY
+    u = (y + z) % NY
+    if cycle == 0:
+        return NY * z + u
+    return NY * ((3 * (z - u + NZ)) % NZ) + u
+
+
+def ring_col(cycle, place):
+    place = (place + NCOL) % NCOL
+    q, u = place // NY, place % NY
+    z = q if cycle == 0 else (3 * q + u) % NZ
+    return z * NY + (u - z + NZ) % NY
+
+
+class Rings:
+    def __init__(self, col, row, parts, send_sems, recv_sems):
+        self.row, self.parts, self.send_sems, self.recv_sems = row, parts, send_sems, recv_sems
+        sign = 1 - 2 * (row % 2)
+        self.lanes = []
+        for cycle in range(2):
+            place = ring_place(cycle, col)
+            for way in range(2):
+                step_dir = sign if way == 0 else -sign
+                self.lanes.append((cycle, way, place, step_dir, ring_col(cycle, place + step_dir)))
+
+    def copies(self, lane, step):
+        cycle, way, place, step_dir, peer = self.lanes[lane]
+        origin = ring_col(cycle, place - step_dir * step)
+        return [
+            pltpu.make_async_remote_copy(
+                src_ref=part(cycle, origin), dst_ref=part(cycle, origin),
+                send_sem=self.send_sems.at[lane, step, k], recv_sem=self.recv_sems.at[lane, step, k],
+                device_id=(peer, self.row), device_id_type=MESH)
+            for k, part in enumerate(self.parts)
+        ]
+
+    def n_steps(self, lane):
+        return LONG - self.lanes[lane][1]
+
+    def start(self, step):
+        for lane in range(4):
+            def go(lane=lane):
+                for copy in self.copies(lane, step):
+                    copy.start()
+            if isinstance(step, int):
+                go()
+            else:
+                pl.when(step < self.n_steps(lane))(go)
+
+    def wait_recv(self, step):
+        for lane in range(4):
+            def go(lane=lane):
+                for copy in self.copies(lane, step):
+                    copy.wait_recv()
+            if isinstance(step, int):
+                if step < self.n_steps(lane):
+                    go()
+            else:
+                pl.when(step < self.n_steps(lane))(go)
+
+    def wait_sends(self):
+        for lane in range(4):
+            @pl.loop(0, self.n_steps(lane))
+            def _(step, lane=lane):
+                for copy in self.copies(lane, step):
+                    copy.wait_send()
+
+
+def exchange_kernel(dy_ref, wn_ref, wa_ref, dxn_ref, dxa_ref, dy_all, wn_all, wa_all, acc_n, acc_a,
+                    ring_send, ring_recv, local_sem, a2a_sems, x_send, x_recv):
+    col, row = lax.axis_index('col'), lax.axis_index('row')
+    x, core = row // 2, row % 2
+    slice_len = dy_ref.shape[0] // NCOL
+    sub = slice_len // NROW
+    nn, na = wn_ref.shape[0], wa_ref.shape[0]
+    width = dy_ref.shape[1]
+    pad_n, pad_a = width - nn, wa_all.shape[1] - na
+
+    own_w = [pltpu.make_async_copy(wn_ref, wn_all.at[col, pl.ds(0, nn)], local_sem.at[0]),
+             pltpu.make_async_copy(wa_ref, wa_all.at[col, pl.ds(pad_a, na)], local_sem.at[1])]
+    for copy in own_w:
+        copy.start()
+
+    def a2a(peer):
+        tokens = pl.ds(pl.multiple_of(peer * slice_len + row * sub, sub), sub)
+        return dy_ref.at[tokens], dy_all.at[row, col]
+
+    for copy in own_w:
+        copy.wait()
+    rings = Rings(col, row, [
+        lambda cycle, origin: wn_all.at[origin, pl.ds(cycle * (nn // 2), nn // 2)],
+        lambda cycle, origin: wa_all.at[origin, pl.ds(pad_a + cycle * (na // 2), na // 2)]], ring_send, ring_recv)
+    rings.start(0)
+
+    src, dst = a2a(col)
+    pltpu.make_async_copy(src, dst, a2a_sems.at[1]).start()
+
+    @pl.loop(1, NCOL)
+    def _(shift):
+        peer = (col + shift) % NCOL
+        src, dst = a2a(peer)
+        pltpu.make_async_remote_copy(src_ref=src, dst_ref=dst, send_sem=a2a_sems.at[0], recv_sem=a2a_sems.at[1],
+                                     device_id=(peer, row), device_id_type=MESH).start()
+
+    wn_all[:, pl.ds(nn, pad_n), :] = jnp.zeros((NCOL, pad_n, wn_all.shape[2]), BF16)
+    wa_all[:, pl.ds(0, pad_a), :] = jnp.zeros((NCOL, pad_a, wa_all.shape[2]), BF16)
+
+    def row_of(dx):
+        return ((x + dx + NX) % NX) * 2 + core
+
+    partner = x * 2 + 1 - core
+    half = NCOL // 2
+
+    def hop(k, slot, target, cols=None):
+        ref = dy_all.at[slot] if cols is None else dy_all.at[slot, cols]
+        return pltpu.make_async_remote_copy(src_ref=ref, dst_ref=ref, send_sem=x_send.at[k], recv_sem=x_recv.at[k],
+                                            device_id=(col, target), device_id_type=MESH)
+
+    own, prev, succ, far = row, row_of(-1), row_of(1), row_of(2)
+    low, high = pl.ds(0, half), pl.ds(half, half)
+    hops = [
+        hop(0, own, succ), hop(1, own, prev), hop(2, own, partner),
+        hop(3, prev, succ, low), hop(4, prev, partner),
+        hop(5, succ, prev, high), hop(6, succ, partner),
+        hop(7, far, partner, low), hop(8, far, partner, high)]
+
+    def ring_steps(first, last):
+        @pl.loop(first, last)
+        def _(step):
+            rings.wait_recv(step - 1)
+            rings.start(step)
+
+    ring_steps(1, 4)
+    pltpu.make_async_copy(dy_all.at[row], dy_all.at[row], a2a_sems.at[1]).wait()
+    for k in (0, 1, 2):
+        hops[k].start()
+    ring_steps(4, 11)
+    hops[0].wait_recv()
+    hops[3].start()
+    hops[4].start()
+    hops[1].wait_recv()
+    hops[5].start()
+    hops[6].start()
+    ring_steps(11, LONG)
+    hops[3].wait_recv()
+    hops[7].start()
+    hops[5].wait_recv()
+    hops[8].start()
+    rings.wait_recv(LONG - 1)
+    for k in (2, 4, 6, 7, 8):
+        hops[k].wait_recv()
+
+    tokens = NROW * sub
+    lo = (nn // 128) * 128
+
+    @pl.loop(0, NCOL // 2)
+    def _(pair):
+        j = pair * 2
+        d0 = dy_all[:, j, :, :].reshape(tokens, width)
+        d1 = dy_all[:, j + 1, :, :].reshape(tokens, width)
+        part_n = (jnp.dot(jnp.concatenate([d0, d1], axis=1), wn_all[pl.ds(j, 2)].reshape(2 * width, wn_all.shape[2]),
+                          preferred_element_type=F32))
+        part_a = jnp.dot(jnp.concatenate([d0[:, lo:], d1[:, lo:]], axis=1),
+                         wa_all[pl.ds(j, 2)].reshape(2 * wa_all.shape[1], wa_all.shape[2]), preferred_element_type=F32)
+
+        @pl.when(pair == 0)
+        def _():
+            acc_n[...] = part_n
+            acc_a[...] = part_a
+
+        @pl.when(pair > 0)
+        def _():
+            acc_n[...] += part_n
+            acc_a[...] += part_a
+
+    dxn_ref[...] = acc_n[...].astype(BF16)
+    dxa_ref[...] = acc_a[...].astype(BF16)
+
+    for k in range(9):
+        hops[k].wait_send()
+    sent = dy_all.at[row, pl.ds(0, NCOL - 1)]
+    pltpu.make_async_copy(sent, sent, a2a_sems.at[0]).wait()
+    rings.wait_sends()
+
+
+def exchange(dy, wn, wa):
+    tokens = dy.shape[0] // NCOL
+    width = dy.shape[1]
+    vmem = pl.BlockSpec(memory_space=pltpu.VMEM)
+    pad_rows = width - (wn.shape[0] // 128) * 128
+    return pl.pallas_call(
+        exchange_kernel,
+        out_shape=(jax.ShapeDtypeStruct((tokens, wn.shape[1]), BF16), jax.ShapeDtypeStruct((tokens, wa.shape[1]), BF16)),
+        in_specs=[pl.BlockSpec(memory_space=pl.ANY), vmem, vmem],
+        out_specs=(vmem, vmem),
+        scratch_shapes=[
+            pltpu.VMEM((NROW, NCOL, tokens // NROW, width), BF16),
+            pltpu.VMEM((NCOL, width, wn.shape[1]), BF16),
+            pltpu.VMEM((NCOL, pad_rows, wa.shape[1]), BF16),
+            pltpu.VMEM((tokens, wn.shape[1]), F32),
+            pltpu.VMEM((tokens, wa.shape[1]), F32),
+            pltpu.SemaphoreType.DMA((4, LONG, 2)),
+            pltpu.SemaphoreType.DMA((4, LONG, 2)),
+            pltpu.SemaphoreType.DMA((2,)),
+            pltpu.SemaphoreType.DMA((2,)),
+            pltpu.SemaphoreType.DMA((9,)),
+            pltpu.SemaphoreType.DMA((9,)),
+        ],
+        compiler_params=pltpu.CompilerParams(has_side_effects=True, vmem_limit_bytes=60 * 1024 * 1024),
+        name='exchange',
+    )(dy, wn, wa)
 
 
 def factored_step(w_loc, grad_loc, r_loc, c_loc, hyper_params, m_total, n_total):
@@ -28,10 +249,6 @@
     return lax.dot_general(activations, grad_out, (((0,), (0,)), ((), ())), preferred_element_type=jnp.float32)
 
 
-def input_grad(grad_out, weight):
-    return lax.dot_general(grad_out, weight.astype(jnp.bfloat16), (((1,), (1,)), ((), ())), preferred_element_type=jnp.float32)
-
-
 def solution(mesh):
     row_size = mesh.shape['row']
     col_size = mesh.shape['col']
@@ -44,11 +261,16 @@
     def body(w_gate, w_up, w_down, x_norm, x_act, dy_gate, dy_up, dy_down, r_gate, c_gate, r_up, c_up, r_down, c_down, hyper_params):
         d_model = w_gate.shape[0] * row_size
         d_ff = w_gate.shape[1] * col_size
+        dy = jnp.concatenate([dy_gate, dy_up, dy_down], axis=1)
+        wn = jnp.concatenate([w_gate.astype(BF16).T, w_up.astype(BF16).T], axis=0)
+        wa = w_down.astype(BF16).T
+        dxn, dxa = exchange(dy, wn, wa)
+        dxn, dxa, x_norm, x_act = lax.optimization_barrier((dxn, dxa, x_norm, x_act))
+        dx_act = lax.all_gather(dxa, 'col', axis=0, tiled=True)
+        dx_norm = lax.all_gather(dxn, 'col', axis=0, tiled=True)
         new_gate, r_gate_new, c_gate_new = factored_step(w_gate, weight_grad(x_norm, dy_gate), r_gate, c_gate, hyper_params, d_model, d_ff)
         new_up, r_up_new, c_up_new = factored_step(w_up, weight_grad(x_norm, dy_up), r_up, c_up, hyper_params, d_model, d_ff)
         new_down, r_down_new, c_down_new = factored_step(w_down, weight_grad(x_act, dy_down), r_down, c_down, hyper_params, d_ff, d_model)
-        dx_norm = lax.psum(input_grad(dy_gate, w_gate) + input_grad(dy_up, w_up), 'col').astype(jnp.bfloat16)
-        dx_act = lax.psum(input_grad(dy_down, w_down), 'col').astype(jnp.bfloat16)
         return (new_gate, new_up, new_down, r_gate_new, c_gate_new, r_up_new, c_up_new, r_down_new, c_down_new, dx_norm, dx_act)
 
     return jax.shard_map(body, mesh=mesh, in_specs=in_specs, out_specs=out_specs, check_vma=False)

time: 1440 us -> 487 us (0.34)
  blocking collectives: 1360 us -> 165 us
  Pallas kernels: 0 us -> 145 us
  waiting for transfers between devices: 0 us -> 53.2 us
  local copies, waits for them, and re-layouts: 3.33 us -> 49.7 us
  matrix products: 54.5 us -> 17.9 us
  other arithmetic: 10.3 us -> 30 us
    psum x1, blocking collectives: 1270 us -> 61.6 us  [factored_step(): row_sum = lax.psum(jnp.sum(grad_sq, axis=1), 'col')]
    pallas_call x0 -> x1, Pallas kernels: none -> 145 us  [exchange(): pl.pallas_call(exchange_kernel, out_shape=(jax.ShapeDtypeStruct((tokens,...]
    all_gather x0 -> x2, waiting for transfers between devices: none -> 52.5 us  [the longest x1 52.5 us: body(): dx_act = lax.all_gather(dxa, 'col', axis=0, tiled=True)]
    unnamed x42 -> x53, local copies, waits for them, and re-layouts: 2.67 us -> 49.1 us
    dot_general x3 -> x0, matrix products: 41.5 us -> none  [input_grad(): lax.dot_general(grad_out, weight.astype(jnp.bfloat16), (((1,), (1,)), (()...]
    concatenate x0 -> x2, other arithmetic: none -> 16.9 us  [the longest x1 16.2 us: body(): dy = jnp.concatenate([dy_gate, dy_up, dy_down], axis=1)]
  transfers between devices with their start and end apart: 0 -> 2, of which waited for: 0 -> 1; matrix products, arithmetic and copies ran while one was open for 0% -> 6% of each run, Pallas kernels for 0% -> 0%
where the time goes in v1:
time: 487 us; the launch traced here: 486 us
  blocking collectives  165 us (34%)
  Pallas kernels  145 us (30%)
  waiting for transfers between devices  53.2 us (11%)
  local copies, waits for them, and re-layouts  49.7 us (10%)
  other arithmetic  30 us (6%)
  between operations  25 us (5%)
  matrix products  17.9 us (4%)
    pallas_call x1, Pallas kernels, exchange(): pl.pallas_call(exchange_kernel, out_shape=(jax.ShapeDtypeStruct((tokens,...  145 us
    psum x1, blocking collectives, factored_step(): u_sq = lax.psum(jnp.sum(update * update), ('row', 'col'))  75.3 us
    psum x1, blocking collectives, factored_step(): row_sum = lax.psum(jnp.sum(grad_sq, axis=1), 'col')  61.6 us
    all_gather x1, waiting for transfers between devices, body(): dx_act = lax.all_gather(dxa, 'col', axis=0, tiled=True)  52.5 us
    unnamed x53, local copies, waits for them, and re-layouts  49.1 us
    psum x1, blocking collectives, factored_step(): r_mean = lax.psum(jnp.sum(r_new), 'row') / m_total  28.5 us
    dot_general x3, matrix products, weight_grad(): lax.dot_general(activations, grad_out, (((0,), (0,)), ((), ())), preferre...  17.9 us
    concatenate x1, other arithmetic, body(): dy = jnp.concatenate([dy_gate, dy_up, dy_down], axis=1)  16.2 us
  transfers between devices with their start and end apart: 2, of which 1 were waited for; matrix products, arithmetic and copies ran while one was open for 6% of the time, Pallas kernels for 0%

profile of v1, /device:TPU:1, one launch (start us, length us, event | category | flops | bytes accessed | tf_op | source)
XLA Modules:
  0.0 486.3 jit_solution(11379708058802836606)
XLA Ops:
  7.2 0.0 all-gather.3.cloned.1.call-start
  7.2 2.2 multiply_reduce_fusion.1
  9.5 9.7 %copy.26 = bf16[16384,160]{1,0:T(8,128)(2,1)} copy(bf16[16384,160]{0,1:T(8,128)(2,1)} %param.20) | data formatting | bytes 10485760 | tf_op args[5]
  19.1 9.8 %copy.27 = bf16[16384,160]{1,0:T(8,128)(2,1)} copy(bf16[16384,160]{0,1:T(8,128)(2,1)} %param.21) | data formatting | bytes 10485760 | tf_op args[6]
  28.9 3.2 copy.28
  32.1 0.7 multiply_reduce_fusion.3
  32.9 0.7 pad_maximum_fusion.1.wn_ref
  33.5 16.2 %pad_maximum_fusion.dy_ref = bf16[16384,384]{1,0:T(8,128)(2,1)} fusion(bf16[16384,64]{1,0:T(8,128)(2,1)} %copy.28, bf16[16384,160]{1,0:T(8,128)(2,1)} %copy.27, bf16[16384,160]{1,0:T(8,128)(2,1)} %copy.26), kind=kLoop, calls=%fused_computation | loop fusion | flops 37748736 | bytes 25165824 | tf_op jit(solution)/shard_map/concatenate | solution.py:264
  49.7 145.1 %exchange.1 = (bf16[512,256]{1,0:T(8,128)(2,1)}, bf16[512,640]{1,0:T(8,128)(2,1)}) custom-call(bf16[16384,384]{1,0:T(8,128)(2,1)} %pad_maximum_fusion.dy_ref, bf16[320,256]{1,0:T(8,128)(2,1)} %pad_maximum_fusion.1.wn_ref, bf16[64,640]{1,0:T(8,128)(2,1)} %get-tuple-element.51.wa_ref), custom_call_target="tpu_custom_call" | custom-call | tf_op jit(solution)/shard_map/exchange/pallas_call | solution.py:208
  194.8 0.0 all-gather.3.cloned.1.call-update
  194.8 0.0 all-gather.5.cloned.1.call-start
  194.8 0.7 all-gather.5.cloned.1.call-update
  195.6 0.6 fusion.9
  196.8 0.0 slice-start.6
  196.8 0.0 slice-start
  196.8 0.0 slice-start.1
  196.8 0.0 slice-start.2
  196.9 6.7 %fusion.2 = (f32[160]{0:T(256)S(1)}, f32[256]{0:T(256)S(1)}, f32[256,160]{0,1:T(8,128)S(1)}) fusion(bf16[16384,160]{0,1:T(8,128)(2,1)} %param.21, bf16[16384,256]{1,0:T(8,128)(2,1)} %param.18), kind=kOutput, calls=%fused_computation.19 | convolution fusion | flops 1342340736 | bytes 13796992 | tf_op jit(solution)/shard_map/dot_general | solution.py:249
  203.6 0.0 slice-start.3
  203.6 0.0 slice-start.4
  203.6 5.8 %fusion = (f32[160]{0:T(256)S(1)}, f32[256]{0:T(256)S(1)}, f32[256,160]{0,1:T(8,128)S(1)}) fusion(bf16[16384,160]{0,1:T(8,128)(2,1)S(1)} %bitcast.18, bf16[16384,256]{1,0:T(8,128)(2,1)} %param.18), kind=kOutput, calls=%fused_computation.17 | convolution fusion | flops 1342340736 | bytes 13796992 | tf_op jit(solution)/shard_map/dot_general | solution.py:249
  209.5 0.9 slice-done.3
  210.4 1.2 slice-done.4
  211.6 0.0 copy-start.15
  211.6 0.0 copy-start.16
  211.6 0.0 copy-start.3
  211.7 5.3 %fusion.4 = (f32[64]{0:T(128)S(1)}, f32[640]{0:T(1024)S(1)}, f32[640,64]{0,1:T(8,128)S(1)}) fusion(bf16[16384,64]{0,1:T(8,128)(2,1)} %param.22, bf16[16384,640]{1,0:T(8,128)(2,1)S(1)} %bitcast.16), kind=kOutput, calls=%fused_computation.21 | convolution fusion | flops 1342340480 | bytes 23235328 | tf_op jit(solution)/shard_map/dot_general | solution.py:249
  217.0 61.6 %all-reduce.1 = (f32[256]{0:T(256)S(1)}, f32[256]{0:T(256)S(1)}, f32[640]{0:T(1024)S(1)}) all-reduce(f32[256]{0:T(256)S(1)} %get-tuple-element.28, f32[256]{0:T(256)S(1)} %get-tuple-element.26, f32[640]{0:T(1024)S(1)} %get-tuple-element.24), channel_id=1, replica_groups=mesh['col'=32,'row'=8] {'col'}, use_global_device_ids=true, to_apply=%region_3.0 | all-reduce | flops 1152 | bytes 9216 | tf_op jit(solution)/shard_map/psum | solution.py:234
  278.6 1.2 fusion.7
  279.8 1.2 fusion.8
  281.1 1.2 fusion.6
  282.3 28.5 %all-reduce.2 = (f32[]{:T(128)}, f32[160]{0:T(256)S(1)}, f32[]{:T(128)}, f32[160]{0:T(256)S(1)}, f32[]{:T(128)}, /*index=5*/f32[64]{0:T(128)S(1)}) all-reduce(f32[]{:T(128)} %get-tuple-element.48, f32[160]{0:T(256)S(1)} %get-tuple-element.27, f32[]{:T(128)} %get-tuple-element.46, ...), channel_id=1, replica_groups=mesh['col'=32,'row'=8] {'row'}, use_global_device_ids=true, to_apply=%region_7.0 | all-reduce | flops 387 | bytes 3096 | tf_op jit(solution)/shard_map/psum | solution.py:238
  312.8 0.7 multiply_add_fusion.4
  313.4 0.0 copy-start.7
  313.5 0.7 multiply_reduce_fusion.2
  314.2 0.6 multiply_add_fusion.6
  314.8 0.0 copy-start.8
  314.9 0.7 multiply_reduce_fusion.4
  315.6 0.6 multiply_add_fusion.8
  316.2 0.0 copy-start.10
  316.2 0.7 multiply_reduce_fusion
  317.0 75.3 %all-reduce = (f32[]{:T(128)}, f32[]{:T(128)}, f32[]{:T(128)}, f32[]{:T(128)}, f32[]{:T(128)}, /*index=5*/f32[]{:T(128)}) all-reduce(f32[]{:T(128)} %multiply_reduce_fusion.4, f32[]{:T(128)} %get-tuple-element.63, f32[]{:T(128)} %multiply_reduce_fusion.2, f32[]{:T(128)} %get-tuple-element.52, ...), channel_id=1, replica_groups=mesh['col'=32,'row'=8] {'row','col'}, use_global_device_ids=true, to_apply=%region_9.0 | all-reduce | flops 6 | bytes 48 | tf_op jit(solution)/shard_map/psum | solution.py:240
  400.3 0.8 multiply_subtract_fusion.1
  401.1 0.8 multiply_subtract_fusion.2
  401.9 0.8 multiply_subtract_fusion
  402.7 52.5 %all-gather.5.cloned.1.call-done = bf16[16384,640]{1,0:T(8,128)(2,1)} async-done(((bf16[512,640]{1,0:T(8,128)(2,1)}), bf16[16384,640]{1,0:T(8,128)(2,1)}) %all-gather.5.cloned.1.call-update) | async-done | bytes 20971536 | tf_op jit(solution)/shard_map/all_gather | solution.py:269
  455.2 7.1 %copy.31 = bf16[16384,256]{1,0:T(8,128)(2,1)} copy(bf16[16384,256]{1,0:T(8,128)(2,1)} %all-gather.3.cloned.1.call-done) | data formatting | bytes 16777216
  462.3 17.2 %copy.32 = bf16[16384,640]{1,0:T(8,128)(2,1)} copy(bf16[16384,640]{1,0:T(8,128)(2,1)} %all-gather.5.cloned.1.call-done) | data formatting | bytes 41943040
  (37 shorter events, 0.1 us)
Async XLA Ops:
  7.2 395.5 %all-gather.3.cloned.1.call-start = ((), (), s32[]{:S(2)}) async-start(), calls=%async_computation | async-start | bytes 8650752 | tf_op jit(solution)/shard_map/all_gather | solution.py:270
  19.1 9.8 %copy-start = (bf16[16384,64]{0,1:T(8,128)(2,1)S(1)}, bf16[16384,64]{0,1:T(8,128)(2,1)}, u32[]{:S(2)}) copy-start(bf16[16384,64]{0,1:T(8,128)(2,1)} %param.22) | copy-start | bytes 6291460
  19.1 13.0 %copy-start.1 = (f32[256,160]{0,1:T(8,128)S(1)}, f32[256,160]{0,1:T(8,128)}, u32[]{:S(2)}) copy-start(f32[256,160]{0,1:T(8,128)} %param.16) | copy-start | bytes 491524
  19.1 13.0 %copy-start.2 = (f32[256,160]{0,1:T(8,128)S(1)}, f32[256,160]{0,1:T(8,128)}, u32[]{:S(2)}) copy-start(f32[256,160]{0,1:T(8,128)} %param.15) | copy-start | bytes 491524
  49.7 145.8 %copy-start.9 = (f32[3]{0:T(128)S(1)}, f32[3]{0:T(128)}, u32[]{:S(2)}) copy-start(f32[3]{0:T(128)} %param.29) | copy-start | bytes 40
  49.7 153.9 %slice-start.5 = ((s8[5242880]{0:T(1024)(128)(4,1)}), s8[1048576]{0:T(1024)(128)(4,1)S(1)}, s32[]{:S(2)}) async-start(s8[5242880]{0:T(1024)(128)(4,1)} %bitcast.17), calls=%async_computation.7 | async-start | bytes 2097152
  194.8 260.4 %all-gather.5.cloned.1.call-start = ((), (), s32[]{:S(2)}) async-start(), calls=%async_computation.1 | async-start | bytes 21626880 | tf_op jit(solution)/shard_map/all_gather | solution.py:269
  196.8 6.8 %slice-start.6 = ((s8[5242880]{0:T(1024)(128)(4,1)}), s8[4194304]{0:T(1024)(128)(4,1)S(1)}, s32[]{:S(2)}) async-start(s8[5242880]{0:T(1024)(128)(4,1)} %bitcast.17), calls=%async_computation.8 | async-start | bytes 8388608
  196.8 12.6 %slice-start = ((s8[20971520]{0:T(1024)(128)(4,1)}), s8[4194304]{0:T(1024)(128)(4,1)S(1)}, s32[]{:S(2)}) async-start(s8[20971520]{0:T(1024)(128)(4,1)} %bitcast.15), calls=%async_computation.2 | async-start | bytes 8388608
  196.8 12.6 %slice-start.1 = ((s8[20971520]{0:T(1024)(128)(4,1)}), s8[4194304]{0:T(1024)(128)(4,1)S(1)}, s32[]{:S(2)}) async-start(s8[20971520]{0:T(1024)(128)(4,1)} %bitcast.15), calls=%async_computation.3 | async-start | bytes 8388608
  196.8 12.6 %slice-start.2 = ((s8[20971520]{0:T(1024)(128)(4,1)}), s8[4194304]{0:T(1024)(128)(4,1)S(1)}, s32[]{:S(2)}) async-start(s8[20971520]{0:T(1024)(128)(4,1)} %bitcast.15), calls=%async_computation.4 | async-start | bytes 8388608
  203.6 6.8 %slice-start.3 = ((s8[20971520]{0:T(1024)(128)(4,1)}), s8[4194304]{0:T(1024)(128)(4,1)S(1)}, s32[]{:S(2)}) async-start(s8[20971520]{0:T(1024)(128)(4,1)} %bitcast.15), calls=%async_computation.5 | async-start | bytes 8388608
  203.6 8.0 %slice-start.4 = ((s8[20971520]{0:T(1024)(128)(4,1)}), s8[4194304]{0:T(1024)(128)(4,1)S(1)}, s32[]{:S(2)}) async-start(s8[20971520]{0:T(1024)(128)(4,1)} %bitcast.15), calls=%async_computation.6 | async-start | bytes 8388608
  211.6 67.0 %copy-start.12 = (f32[256]{0:T(256)S(1)}, f32[256]{0:T(256)}, u32[]{:S(2)}) copy-start(f32[256]{0:T(256)} %param.25) | copy-start | bytes 3076
  211.6 68.2 %copy-start.13 = (f32[256]{0:T(256)S(1)}, f32[256]{0:T(256)}, u32[]{:S(2)}) copy-start(f32[256]{0:T(256)} %param.23) | copy-start | bytes 3076
  211.6 69.5 %copy-start.11 = (f32[640]{0:T(1024)S(1)}, f32[640]{0:T(1024)}, u32[]{:S(2)}) copy-start(f32[640]{0:T(1024)} %param.27) | copy-start | bytes 7684
  211.6 101.2 %copy-start.14 = (f32[160]{0:T(256)S(1)}, f32[160]{0:T(256)}, u32[]{:S(2)}) copy-start(f32[160]{0:T(256)} %param.26) | copy-start | bytes 1924
  211.6 102.6 %copy-start.15 = (f32[160]{0:T(256)S(1)}, f32[160]{0:T(256)}, u32[]{:S(2)}) copy-start(f32[160]{0:T(256)} %param.24) | copy-start | bytes 1924
  211.6 103.9 %copy-start.16 = (f32[64]{0:T(128)S(1)}, f32[64]{0:T(128)}, u32[]{:S(2)}) copy-start(f32[64]{0:T(128)} %param.28) | copy-start | bytes 772
  211.6 190.2 %copy-start.3 = (f32[640,64]{0,1:T(8,128)S(1)}, f32[640,64]{0,1:T(8,128)}, u32[]{:S(2)}) copy-start(f32[640,64]{0,1:T(8,128)} %param.17) | copy-start | bytes 491524
  279.8 182.5 %copy-start.5 = (f32[256]{0:T(256)}, f32[256]{0:T(256)S(1)}, u32[]{:S(2)}) copy-start(f32[256]{0:T(256)S(1)} %get-tuple-element.80) | copy-start | bytes 3076
  281.1 181.2 %copy-start.6 = (f32[256]{0:T(256)}, f32[256]{0:T(256)S(1)}, u32[]{:S(2)}) copy-start(f32[256]{0:T(256)S(1)} %get-tuple-element.78) | copy-start | bytes 3076
  282.3 180.0 %copy-start.4 = (f32[640]{0:T(1024)}, f32[640]{0:T(1024)S(1)}, u32[]{:S(2)}) copy-start(f32[640]{0:T(1024)S(1)} %get-tuple-element.82) | copy-start | bytes 7684
  313.4 148.9 %copy-start.7 = (f32[160]{0:T(256)}, f32[160]{0:T(256)S(1)}, u32[]{:S(2)}) copy-start(f32[160]{0:T(256)S(1)} %multiply_add_fusion.4) | copy-start | bytes 1924
  314.8 147.5 %copy-start.8 = (f32[160]{0:T(256)}, f32[160]{0:T(256)S(1)}, u32[]{:S(2)}) copy-start(f32[160]{0:T(256)S(1)} %multiply_add_fusion.6) | copy-start | bytes 1924
  316.2 146.1 %copy-start.10 = (f32[64]{0:T(128)}, f32[64]{0:T(128)S(1)}, u32[]{:S(2)}) copy-start(f32[64]{0:T(128)S(1)} %multiply_add_fusion.8) | copy-start | bytes 772
Sparse Core Ops, SparseCore 0:
  194.9 99.0 all-gather.2
  296.6 158.5 all-gather.4

commit v2 on v0

v2 whole, which is shorter than its diff:
```python
import jax
import jax.numpy as jnp
from jax import lax
from jax.experimental import pallas as pl
from jax.experimental.pallas import tpu as pltpu
from jax.sharding import PartitionSpec as P

EPS_ONE = 1e-30
EPS_TWO = 1e-3
MESH = pl.DeviceIdType.MESH
NY, NZ, NX = 4, 8, 4
NCOL, NROW = NY * NZ, NX * 2
LONG = NCOL // 2
BF16, F32 = jnp.bfloat16, jnp.float32


def ring_place(cycle, col):
    y, z = col % NY, col // NY
    u = (y + z) % NY
    if cycle == 0:
        return NY * z + u
    return NY * ((3 * (z - u + NZ)) % NZ) + u


def ring_col(cycle, place):
    place = (place + NCOL) % NCOL
    q, u = place // NY, place % NY
    z = q if cycle == 0 else (3 * q + u) % NZ
    return z * NY + (u - z + NZ) % NY


class Rings:
    def __init__(self, col, row, parts, send_sems, recv_sems):
        self.row, self.parts, self.send_sems, self.recv_sems = row, parts, send_sems, recv_sems
        sign = 1 - 2 * (row % 2)
        self.lanes = []
        for cycle in range(2):
            place = ring_place(cycle, col)
            for way in range(2):
                step_dir = sign if way == 0 else -sign
                self.lanes.append((cycle, way, place, step_dir, ring_col(cycle, place + step_dir)))

    def copy(self, lane, step, k):
        cycle, way, place, step_dir, peer = self.lanes[lane]
        ref = self.parts[k](cycle, ring_col(cycle, place - step_dir * step))
        return pltpu.make_async_remote_copy(
            src_ref=ref, dst_ref=ref, send_sem=self.send_sems.at[lane, k], recv_sem=self.recv_sems.at[lane, step, k],
            device_id=(peer, self.row), device_id_type=MESH)

    def start(self, step):
        for k in range(len(self.parts)):
            for lane in range(4):
                self.guard(lane, step, lambda lane=lane, k=k: self.copy(lane, step, k).start())

    def guard(self, lane, step, go):
        n_steps = LONG - self.lanes[lane][1]
        if isinstance(step, int):
            if step < n_steps:
                go()
        else:
            pl.when(step < n_steps)(go)

    def wait_recv(self, step):
        for k in range(len(self.parts)):
            for lane in range(4):
                self.guard(lane, step, lambda lane=lane, k=k: self.copy(lane, step, k).wait_recv())

    def forward(self, step):
        for k in range(len(self.parts)):
            for lane in range(4):
                self.guard(lane, step - 1, lambda lane=lane, k=k: self.copy(lane, step - 1, k).wait_recv())
                self.guard(lane, step, lambda lane=lane, k=k: self.copy(lane, step, k).start())

    def wait_sends(self, totals):
        for lane in range(4):
            for k, total in enumerate(totals):
                ref = total(LONG - self.lanes[lane][1])
                pltpu.make_async_copy(ref, ref, self.send_sems.at[lane, k]).wait()


def step_kernel(dyg_ref, dyu_ref, dyd_ref, xn_ref, xa_ref, wn_ref, wa_ref, wg_ref, wu_ref, wd_ref, r_ref, c_ref, hyper_ref,
                wg_out, wu_out, wd_out, r_out, c_out, dxn_ref, dxa_ref,
                dn_all, dd_all, wn_all, wa_all, acc_n, acc_a, own_n, own_a,
                xn_buf, xa_buf, dyn_buf, dyd_buf, grad_n, grad_d,
                col_msg, row_msg, u_msg, r_msg, z_msg,
                w_send, w_recv, ag_send, ag_recv, local_sem, a2a_sems, x_send, x_recv, tile_sems, st_send, st_recv):
    col, row = lax.axis_index('col'), lax.axis_index('row')
    x, core = row // 2, row % 2
    tokens = dxn_ref.shape[0] // NCOL
    quarter = tokens // NX
    ng = dyg_ref.shape[0]
    nd = dyd_ref.shape[0]
    nn = 2 * ng
    hd = nd // 2
    fetch_own = [pltpu.make_async_copy(wn_ref, wn_all.at[col], local_sem.at[0]),
                 pltpu.make_async_copy(wa_ref, wa_all.at[col], local_sem.at[1])]

    w_rings = Rings(col, row, [
        lambda cycle, origin: wn_all.at[origin, pl.ds(cycle * ng, ng)],
        lambda cycle, origin: wa_all.at[origin, pl.ds(cycle * hd, hd)]], w_send, w_recv)
    if DO_W:
        for copy in fetch_own:
            copy.start()
        for copy in fetch_own:
            copy.wait()
        w_rings.start(0)

    rows_n, rows_d = pl.ds(core * ng, ng), pl.ds(core * hd, hd)

    def a2a(src):
        @pl.loop(0, NCOL)
        def _(shift):
            peer = (col + shift) % NCOL
            cols = pl.ds(pl.multiple_of(peer * tokens + x * quarter, quarter), quarter)
            pieces = ((src.at[:, cols], dn_all.at[x, col, rows_n]), (dyd_ref.at[rows_d, cols], dd_all.at[x, col, rows_d]))

            @pl.when(shift == 0)
            def _():
                for k, (s, d) in enumerate(pieces):
                    pltpu.make_async_copy(s, d, a2a_sems.at[1, k]).start()

            @pl.when(shift > 0)
            def _():
                for k, (s, d) in enumerate(pieces):
                    pltpu.make_async_remote_copy(src_ref=s, dst_ref=d, send_sem=a2a_sems.at[0, k], recv_sem=a2a_sems.at[1, k],
                                                 device_id=(peer, row), device_id_type=MESH).start()

    if DO_A2A:
        pl.when(core == 0)(lambda: a2a(dyg_ref))
        pl.when(core == 1)(lambda: a2a(dyu_ref))

    def x_of(dx):
        return (x + dx + NX) % NX

    half = NCOL // 2
    every, low, high = pl.ds(0, NCOL), pl.ds(0, half), pl.ds(half, half)
    own, prev, succ, far = x, x_of(-1), x_of(1), x_of(2)
    partner = x * 2 + 1 - core

    class Hop:
        def __init__(self, k, slot, target, cols=every):
            refs = (dn_all.at[slot, cols, rows_n], dd_all.at[slot, cols, rows_d])
            self.copies = [pltpu.make_async_remote_copy(
                src_ref=ref, dst_ref=ref, send_sem=x_send.at[k, p], recv_sem=x_recv.at[k, p],
                device_id=(col, target), device_id_type=MESH) for p, ref in enumerate(refs)]

        def start(self):
            for copy in self.copies:
                copy.start()

        def wait_recv(self):
            for copy in self.copies:
                copy.wait_recv()

        def wait_send(self):
            for copy in self.copies:
                copy.wait_send()

    to_succ, to_prev = succ * 2 + core, prev * 2 + core
    hops = [
        Hop(0, own, to_succ), Hop(1, own, to_prev), Hop(2, own, partner),
        Hop(3, prev, to_succ, low), Hop(4, prev, partner),
        Hop(5, succ, to_prev, high), Hop(6, succ, partner),
        Hop(7, far, partner, low), Hop(8, far, partner, high)]

    def w_steps(first, last):
        if DO_W:
            @pl.loop(first, last)
            def _(step):
                w_rings.forward(step)

    w_steps(1, W_A)
    if DO_A2A:
        for k, ref in enumerate((dn_all.at[x, every, rows_n], dd_all.at[x, every, rows_d])):
            pltpu.make_async_copy(ref, ref, a2a_sems.at[1, k]).wait()
    if DO_X:
        for k in (0, 1, 2):
            hops[k].start()
    w_steps(W_A, W_B)
    if DO_X:
        hops[0].wait_recv()
        hops[3].start()
        hops[4].start()
        hops[1].wait_recv()
        hops[5].start()
        hops[6].start()
    w_steps(W_B, LONG)
    if DO_W:
        w_rings.wait_recv(LONG - 1)
    if DO_X:
        hops[3].wait_recv()
        hops[7].start()
        hops[5].wait_recv()
        hops[8].start()
        for k in (2, 4, 6, 7, 8):
            hops[k].wait_recv()

    group = 4
    if DO_MM:
        @pl.loop(0, NCOL // group)
        def _(g):
            js = pl.ds(g * group, group)
            lhs_n = jnp.concatenate([dn_all[q, js].reshape(group * nn, quarter) for q in range(NX)], axis=1)
            lhs_d = jnp.concatenate([dd_all[q, js].reshape(group * nd, quarter) for q in range(NX)], axis=1)
            dims = (((0,), (0,)), ((), ()))
            part_n = lax.dot_general(lhs_n, wn_all[js].reshape(group * nn, wn_all.shape[2]), dims, preferred_element_type=F32)
            part_a = lax.dot_general(lhs_d, wa_all[js].reshape(group * nd, wa_all.shape[2]), dims, preferred_element_type=F32)

            @pl.when(g == 0)
            def _():
                acc_n[...] = part_n
                acc_a[...] = part_a

            @pl.when(g > 0)
            def _():
                acc_n[...] += part_n
                acc_a[...] += part_a

    own_n[...] = acc_n[...].astype(BF16)
    own_a[...] = acc_a[...].astype(BF16)
    mine = pl.ds(pl.multiple_of(col * tokens, tokens), tokens)
    place_own = [pltpu.make_async_copy(own_n, dxn_ref.at[mine], local_sem.at[0]),
                 pltpu.make_async_copy(own_a, dxa_ref.at[mine], local_sem.at[1])]
    for copy in place_own:
        copy.start()
    for copy in place_own:
        copy.wait()

    def span(ref, offset, count):
        def part(cycle, origin):
            return ref.at[pl.ds(pl.multiple_of(origin * tokens + cycle * (tokens // 2) + offset, 16), count)]
        return part

    sizes = [(dxa_ref, tokens // 4), (dxa_ref, tokens // 4), (dxn_ref, tokens // 2)]
    ag = Rings(col, row, [span(dxa_ref, 0, tokens // 4), span(dxa_ref, tokens // 4, tokens // 4), span(dxn_ref, 0, tokens // 2)],
               ag_send, ag_recv)

    tile = xn_buf.shape[1]
    n_tiles = dxn_ref.shape[0] // tile

    def tile_copies(t, slot):
        at = pl.ds(pl.multiple_of(t * tile, tile), tile)
        pairs = ((xn_ref.at[at], xn_buf.at[slot]), (xa_ref.at[at], xa_buf.at[slot]),
                 (dyg_ref.at[:, at], dyn_buf.at[slot, pl.ds(0, ng)]), (dyu_ref.at[:, at], dyn_buf.at[slot, pl.ds(ng, ng)]),
                 (dyd_ref.at[:, at], dyd_buf.at[slot]))
        return [pltpu.make_async_copy(s, d, tile_sems.at[slot, k]) for k, (s, d) in enumerate(pairs)]

    def dw_tile(t):
        slot = t % 2
        for copy in tile_copies(t, slot):
            copy.wait()

        @pl.when(t + 1 < n_tiles)
        def _():
            for copy in tile_copies(t + 1, 1 - slot):
                copy.start()
        grad_n[...] += jnp.dot(dyn_buf[slot], xn_buf[slot], preferred_element_type=F32)
        grad_d[...] += jnp.dot(dyd_buf[slot], xa_buf[slot], preferred_element_type=F32)

    if DO_AG:
        ag.start(0)
    grad_n[...] = jnp.zeros_like(grad_n)
    grad_d[...] = jnp.zeros_like(grad_d)
    if DO_DW:
        for copy in tile_copies(0, 0):
            copy.start()
    per_step = n_tiles // DW_STEPS

    @pl.loop(1, DW_STEPS + 1)
    def _(step):
        if DO_AG:
            ag.forward(step)
        if DO_DW:
            @pl.loop(0, per_step)
            def _(k):
                dw_tile((step - 1) * per_step + k)

    def ag_step(step):
        if DO_AG:
            ag.forward(step)

    m = xn_ref.shape[1]
    beta_two, rho, clip = hyper_ref[0], hyper_ref[1], hyper_ref[2]
    n_elem = float(m * NROW * ng * NCOL)
    n_rows, n_cols = float(m * NROW), float(ng * NCOL)
    scales = ((n_rows, n_cols), (n_rows, n_cols), (n_cols, n_rows))

    def lanes_of(values):
        lane = lax.broadcasted_iota(jnp.int32, (1, 128), 1)
        out = jnp.zeros((1, 128), F32)
        for k, value in enumerate(values):
            out = jnp.where(lane == k, value, out)
        return out

    def scatter(k, ref, axis):
        count, mine_at = (NCOL, col) if axis == 'col' else (NROW, row)

        @pl.loop(1, count)
        def _(shift):
            peer = (mine_at + shift) % count
            target = (peer, row) if axis == 'col' else (col, peer)
            pltpu.make_async_remote_copy(src_ref=ref.at[mine_at], dst_ref=ref.at[mine_at], send_sem=st_send.at[k],
                                         recv_sem=st_recv.at[k], device_id=target, device_id_type=MESH).start()

    def collect(k, ref, count):
        part = ref.at[pl.ds(0, count - 1)]
        pltpu.make_async_copy(part, part, st_recv.at[k]).wait()

    def drain(k, ref, count):
        part = ref.at[pl.ds(0, count - 1)]
        pltpu.make_async_copy(part, part, st_send.at[k]).wait()

    def pick(vec, k):
        lane = lax.broadcasted_iota(jnp.int32, (1, 128), 1)
        return jnp.sum(jnp.where(lane == k, vec, 0.0))

    def grads():
        return grad_n[pl.ds(0, ng), :], grad_n[pl.ds(ng, ng), :], grad_d[...]

    ag_step(DW_STEPS + 1)
    squares = [g * g + EPS_ONE for g in grads()]
    w_parts = [jnp.sum(w[...] * w[...]) for w in (wg_ref, wu_ref, wd_ref)]
    row_sums = [jnp.sum(s, axis=0, keepdims=True) for s in squares]
    col_sums = jnp.concatenate([jnp.sum(s, axis=1, keepdims=True) for s in squares], axis=0)
    col_msg[col] = jnp.concatenate(row_sums + [lanes_of(w_parts)], axis=1)
    row_msg[row] = jnp.transpose(jnp.broadcast_to(col_sums, (nn + nd, 128)))[0:1, :]
    if DO_ST:
        scatter(0, col_msg, 'col')
        scatter(1, row_msg, 'row')

    ag_step(DW_STEPS + 2)
    if DO_ST:
        collect(0, col_msg, NCOL)
        collect(1, row_msg, NROW)
    r_total = jnp.sum(col_msg[...], axis=0)
    c_total = jnp.sum(row_msg[...], axis=0)
    n_r = r_total.shape[1] - 128
    lane_r = lax.broadcasted_iota(jnp.int32, (1, n_r), 1)
    lane_c = lax.broadcasted_iota(jnp.int32, (1, nn + nd), 1)
    r_new = beta_two * r_ref[...] + (1.0 - beta_two) * (r_total[:, :n_r] / jnp.where(lane_r < 2 * m, n_cols, n_rows))
    c_new = beta_two * c_ref[...] + (1.0 - beta_two) * (c_total / jnp.where(lane_c < nn, n_rows, n_cols))
    r_out[...] = r_new
    c_out[...] = c_new
    r_cuts = ((0, m), (m, 2 * m), (2 * m, n_r))
    r_sums = [jnp.sum(r_new[:, a:b]) for a, b in r_cuts]
    w_line = [pick(r_total[:, n_r:], k) for k in range(3)]
    r_msg[row] = lanes_of(r_sums + w_line)
    if DO_ST:
        scatter(2, r_msg, 'row')

    ag_step(DW_STEPS + 3)
    if DO_ST:
        collect(2, r_msg, NROW)
    totals = jnp.sum(r_msg[...], axis=0)
    c_col = jnp.transpose(jnp.broadcast_to(c_out[...], (128, nn + nd)))[:, 0:1]
    c_cols = (c_col[:ng], c_col[ng:nn], c_col[nn:])
    u_sums = []
    new_refs = (wg_out, wu_out, wd_out)
    for k, g in enumerate(grads()):
        r_mean = pick(totals, k) / scales[k][0]
        r_row = r_out[:, r_cuts[k][0]:r_cuts[k][1]]
        update = g * lax.rsqrt(r_row * c_cols[k] / r_mean)
        new_refs[k][...] = update
        u_sums.append(jnp.sum(update * update))
    w_sq = [pick(totals, 3 + k) for k in range(3)]
    u_msg[row] = lanes_of(u_sums)
    if DO_ST:
        scatter(3, u_msg, 'row')

    ag_step(DW_STEPS + 4)
    if DO_ST:
        collect(3, u_msg, NROW)
    z_msg[col] = jnp.sum(u_msg[...], axis=0)
    if DO_ST:
        scatter(4, z_msg, 'col')

    ag_step(DW_STEPS + 5)
    if DO_ST:
        collect(4, z_msg, NCOL)
    u_total = jnp.sum(z_msg[...], axis=0)

    def rms(value):
        return jnp.sqrt(jnp.full((1, 1), value / n_elem, F32))

    for k, (w, out) in enumerate(zip((wg_ref, wu_ref, wd_ref), new_refs)):
        shrink = jnp.maximum(1.0, rms(pick(u_total, k)) / clip)
        step_size = rho * jnp.maximum(EPS_TWO, rms(w_sq[k]))
        out[...] = w[...] - step_size * (out[...] / shrink)

    @pl.loop(DW_STEPS + 6, LONG)
    def _(step):
        ag_step(step)
    if DO_AG:
        ag.wait_recv(LONG - 1)

    if DO_X:
        for hop in hops:
            hop.wait_send()
    if DO_A2A:
        for k, ref in enumerate((dn_all.at[0, pl.ds(0, NCOL - 1), pl.ds(0, ng)], dd_all.at[0, pl.ds(0, NCOL - 1), pl.ds(0, hd)])):
            pltpu.make_async_copy(ref, ref, a2a_sems.at[0, k]).wait()
    if DO_W:
        w_rings.wait_sends([lambda n: wn_all.at[pl.ds(0, n), pl.ds(0, ng)], lambda n: wa_all.at[pl.ds(0, n), pl.ds(0, hd)]])
    if DO_AG:
        ag.wait_sends([lambda n, ref=ref, size=size: ref.at[pl.ds(0, n * size)] for ref, size in sizes])
    if DO_ST:
        for k, ref, count in ((0, col_msg, NCOL), (1, row_msg, NROW), (2, r_msg, NROW), (3, u_msg, NROW), (4, z_msg, NCOL)):
            drain(k, ref, count)


DO_W = DO_A2A = DO_X = DO_MM = DO_AG = DO_DW = DO_ST = True
W_A, W_B, DW_STEPS = 6, 11, 8
TILE = 512


def fused_step(dyg, dyu, dyd, xn, xa, wn, wa, wg, wu, wd, r_all, c_all, hyper):
    tokens = xn.shape[0] // NCOL
    ng, nd, m, ma = dyg.shape[0], dyd.shape[0], xn.shape[1], xa.shape[1]
    nn = 2 * ng
    vmem, hbm = pl.BlockSpec(memory_space=pltpu.VMEM), pl.BlockSpec(memory_space=pl.ANY)
    smem = pl.BlockSpec(memory_space=pltpu.SMEM)
    dma = pltpu.SemaphoreType.DMA
    shape = jax.ShapeDtypeStruct
    return pl.pallas_call(
        step_kernel,
        out_shape=(shape(wg.shape, F32), shape(wu.shape, F32), shape(wd.shape, F32), shape(r_all.shape, F32), shape(c_all.shape, F32),
                   shape(xn.shape, BF16), shape(xa.shape, BF16)),
        in_specs=[hbm] * 5 + [vmem] * 7 + [smem],
        out_specs=(vmem,) * 5 + (hbm,) * 2,
        scratch_shapes=[
            pltpu.VMEM((NX, NCOL, nn, tokens // NX), BF16),
            pltpu.VMEM((NX, NCOL, nd, tokens // NX), BF16),
            pltpu.VMEM((NCOL, nn, m), BF16),
            pltpu.VMEM((NCOL, nd, ma), BF16),
            pltpu.VMEM((tokens, m), F32),
            pltpu.VMEM((tokens, ma), F32),
            pltpu.VMEM((tokens, m), BF16),
            pltpu.VMEM((tokens, ma), BF16),
            pltpu.VMEM((2, TILE, m), BF16),
            pltpu.VMEM((2, TILE, ma), BF16),
            pltpu.VMEM((2, nn, TILE), BF16),
            pltpu.VMEM((2, nd, TILE), BF16),
            pltpu.VMEM((nn, m), F32),
            pltpu.VMEM((nd, ma), F32),
            pltpu.VMEM((NCOL, 1, 2 * m + ma + 128), F32),
            pltpu.VMEM((NROW, 1, nn + nd), F32),
            pltpu.VMEM((NROW, 1, 128), F32),
            pltpu.VMEM((NROW, 1, 128), F32),
            pltpu.VMEM((NCOL, 1, 128), F32),
            dma((4, 2)), dma((4, LONG, 2)), dma((4, 3)), dma((4, LONG, 3)), dma((2,)), dma((2, 2)), dma((9, 2)), dma((9, 2)),
            dma((2, 5)), dma((5,)), dma((5,)),
        ],
        compiler_params=pltpu.CompilerParams(has_side_effects=True, vmem_limit_bytes=60 * 1024 * 1024),
        name='fused_step',
    )(dyg, dyu, dyd, xn, xa, wn, wa, wg, wu, wd, r_all, c_all, hyper)


def solution(mesh):
    weight_spec = P('row', 'col')
    act_spec = P(None, 'row')
    grad_spec = P(None, 'col')
    in_specs = (weight_spec,) * 3 + (act_spec, act_spec) + (grad_spec,) * 3 + (P('row'), P('col')) * 3 + (P(),)
    out_specs = (weight_spec,) * 3 + (P('row'), P('col')) * 3 + (act_spec, act_spec)

    def body(w_gate, w_up, w_down, x_norm, x_act, dy_gate, dy_up, dy_down, r_gate, c_gate, r_up, c_up, r_down, c_down, hyper_params):
        m, ng = w_gate.shape
        wg, wu, wd = w_gate.T, w_up.T, w_down.T
        wn = jnp.concatenate([wg.astype(BF16), wu.astype(BF16)], axis=0)
        wa = wd.astype(BF16)
        r_all = jnp.concatenate([r_gate, r_up, r_down])[None]
        c_all = jnp.concatenate([c_gate, c_up, c_down])[None]
        wg, wu, wd, r_all, c_all, dx_norm, dx_act = fused_step(
            dy_gate.T, dy_up.T, dy_down.T, x_norm, x_act, wn, wa, wg, wu, wd, r_all, c_all, hyper_params)
        r_all, c_all = r_all[0], c_all[0]
        return (wg.T, wu.T, wd.T, r_all[:m], c_all[:ng], r_all[m:2 * m], c_all[ng:2 * ng], r_all[2 * m:], c_all[2 * ng:],
                dx_norm, dx_act)

    return jax.shard_map(body, mesh=mesh, in_specs=in_specs, out_specs=out_specs, check_vma=False)
```

time: 1440 us -> 348 us (0.24)
  blocking collectives: 1360 us -> 0 us
  Pallas kernels: 0 us -> 306 us
  matrix products: 54.5 us -> 0 us
  local copies, waits for them, and re-layouts: 3.33 us -> 35.3 us
    psum x3 -> x0, blocking collectives: 1360 us -> none  [the longest x1 1270 us: factored_step(): row_sum = lax.psum(jnp.sum(grad_sq, axis=1), 'col')]
    pallas_call x0 -> x1, Pallas kernels: none -> 306 us  [fused_step(): pl.pallas_call(step_kernel, out_shape=(shape(wg.shape, F32), shape(wu.sha...]
    dot_general x6 -> x0, matrix products: 54.5 us -> none  [the longest x3 41.5 us: input_grad(): lax.dot_general(grad_out, weight.astype(jnp.bfloat16), (((1,), (1,)), (()...]
    unnamed x42 -> x5, local copies, waits for them, and re-layouts: 2.67 us -> 29 us
where the time goes in v2:
time: 348 us; the launch traced here: 346 us
  Pallas kernels  306 us (88%)
  local copies, waits for them, and re-layouts  35.3 us (10%)
  other arithmetic  4.76 us (1%)
    pallas_call x1, Pallas kernels, fused_step(): pl.pallas_call(step_kernel, out_shape=(shape(wg.shape, F32), shape(wu.sha...  306 us
    unnamed x5, local copies, waits for them, and re-layouts  29 us

profile of v2, /device:TPU:1, one launch (start us, length us, event | category | flops | bytes accessed | tf_op | source)
XLA Modules:
  0.0 346.5 jit_solution(8146730149287370684)
XLA Ops:
  0.6 0.8 pad_maximum_fusion.2
  1.4 0.6 broadcast_in_dim.7.c_ref
  2.0 0.7 pad_maximum_fusion.1
  2.7 0.6 broadcast_in_dim.6.r_ref
  3.3 1.6 bitcast_convert_fusion.wa_ref
  4.9 1.0 bitcast_convert_fusion.1
  5.9 0.7 pad_maximum_fusion.wn_ref
  6.6 305.8 %fused_step.1 = (f32[160,256]{1,0:T(8,128)}, f32[160,256]{1,0:T(8,128)}, f32[64,640]{1,0:T(8,128)}, f32[1,1152]{1,0:T(1,128)}, f32[1,384]{1,0:T(1,128)}, /*index...) custom-call(bf16[160,16384]{1,0:T(8,128)(2,1)} %bitcast.18, bf16[160,16384]{1,0:T(8,128)(2,1)} %bitcast.19, ...), custom_call_target="tpu_custom_call" | custom-call | tf_op jit(solution)/shard_map/fused_step/pallas_call | solution.py:424
  312.3 1.2 slice_bitcast_fusion
  313.6 1.3 fusion.1
  314.9 1.3 fusion
  316.2 1.3 slice_reduce_fusion
  317.5 1.6 copy.31
  319.0 1.6 copy.32
  320.6 1.6 copy.33
  322.2 7.1 %copy.34 = bf16[16384,256]{1,0:T(8,128)(2,1)} copy(bf16[16384,256]{1,0:T(8,128)(2,1)} %get-tuple-element.51) | data formatting | bytes 16777216
  329.3 17.1 %copy.35 = bf16[16384,640]{1,0:T(8,128)(2,1)} copy(bf16[16384,640]{1,0:T(8,128)(2,1)} %get-tuple-element.52) | data formatting | bytes 41943040

commit v3 on v2

--- a/solution.py
+++ b/solution.py
@@ -78,12 +78,63 @@
                 pltpu.make_async_copy(ref, ref, self.send_sems.at[lane, k]).wait()
 
 
+class Trees:
+    def __init__(self, col, row, pieces, send_sems, recv_sems):
+        self.row, self.pieces, self.send_sems, self.recv_sems = row, pieces, send_sems, recv_sems
+        self.y, self.z, self.sign = col % NY, col // NY, 1 - 2 * (row % 2)
+
+    def at(self, dy, dz):
+        y = (self.y + self.sign * dy + NY) % NY
+        z = (self.z + self.sign * dz + NZ) % NZ
+        return z * NY + y
+
+    def copy(self, tree, k, origin, target):
+        (ey, ez), (fy, fz) = origin, target
+        ref = self.pieces[tree][k](self.at(ey, ez))
+        return pltpu.make_async_remote_copy(
+            src_ref=ref, dst_ref=ref, send_sem=self.send_sems.at[tree, k],
+            recv_sem=self.recv_sems.at[tree, (ey - fy) % NY, (ez - fz) % NZ, k],
+            device_id=(self.at(fy, fz), self.row), device_id_type=MESH)
+
+    @staticmethod
+    def children(tree, ey, ez):
+        along_y = {0: [(1, (0, 1)), (-1, (0, 1))], -1: [(1, (0,))], 1: [(-1, (1,))], 2: []}[ey]
+        if ez == 0:
+            along_z = [1, -1]
+        elif ez < 0:
+            along_z = [1] if ez > -NZ // 2 else []
+        else:
+            along_z = [-1] if ez < NZ // 2 - 1 else []
+        if tree == 0:
+            ys, zs = (along_y if ez == 0 else []), along_z
+        else:
+            ys, zs = along_y, (along_z if ey == 0 else [])
+        return [((0, f), (0, 1)) for f in zs] + [((f, 0), ks) for f, ks in ys]
+
+    def wait(self, tree, k, ey, ez):
+        ref = self.pieces[tree][k](self.at(ey, ez))
+        pltpu.make_async_copy(ref, ref, self.recv_sems.at[tree, ey % NY, ez % NZ, k]).wait()
+
+    def round(self, r):
+        for tree in (1, 0):
+            for ez in (0, -1, 1, -2, 2, -3, 3, -4):
+                for ey in (0, -1, 1, 2):
+                    if abs(ey) + abs(ez) != r:
+                        continue
+                    if r:
+                        for k in range(2):
+                            self.wait(tree, k, ey, ez)
+                    for target, ks in self.children(tree, ey, ez):
+                        for k in ks:
+                            self.copy(tree, k, (ey, ez), target).start()
+
+
 def step_kernel(dyg_ref, dyu_ref, dyd_ref, xn_ref, xa_ref, wn_ref, wa_ref, wg_ref, wu_ref, wd_ref, r_ref, c_ref, hyper_ref,
                 wg_out, wu_out, wd_out, r_out, c_out, dxn_ref, dxa_ref,
-                dn_all, dd_all, wn_all, wa_all, acc_n, acc_a, own_n, own_a,
+                dn_all, dd_all, wn_all, wa_all, acc_n, acc_a,
                 xn_buf, xa_buf, dyn_buf, dyd_buf, grad_n, grad_d,
                 col_msg, row_msg, u_msg, r_msg, z_msg,
-                w_send, w_recv, ag_send, ag_recv, local_sem, a2a_sems, x_send, x_recv, tile_sems, st_send, st_recv):
+                w_send, w_recv, ag_send, ag_recv, local_sem, a2a_sent, a2a_recv, x_send, x_recv, tile_sems, st_send, st_recv):
     col, row = lax.axis_index('col'), lax.axis_index('row')
     x, core = row // 2, row % 2
     tokens = dxn_ref.shape[0] // NCOL
@@ -95,136 +146,143 @@
     fetch_own = [pltpu.make_async_copy(wn_ref, wn_all.at[col], local_sem.at[0]),
                  pltpu.make_async_copy(wa_ref, wa_all.at[col], local_sem.at[1])]
 
-    w_rings = Rings(col, row, [
-        lambda cycle, origin: wn_all.at[origin, pl.ds(cycle * ng, ng)],
-        lambda cycle, origin: wa_all.at[origin, pl.ds(cycle * hd, hd)]], w_send, w_recv)
+    def w_piece(ref, first, count):
+        return lambda origin: ref.at[origin, pl.ds(first, count)]
+
+    w_cuts = (((wn_all, 0, W_CUT), (wa_all, 0, hd)), ((wn_all, W_CUT, nn - W_CUT), (wa_all, hd, hd)))
+    trees = Trees(col, row, [[w_piece(*cut) for cut in cuts] for cuts in w_cuts], w_send, w_recv)
+
+    rows_n, rows_d = pl.ds(core * ng, ng), pl.ds(core * hd, hd)
+
+    def shift_of(t):
+        return ((2 * (t % 2) - 1) * ((t + 1) // 2) + NCOL) % NCOL
+
+    def a2a_pieces(src, t, peer):
+        cols = pl.ds(pl.multiple_of(peer * tokens + x * quarter, quarter), quarter)
+        return (src.at[:, cols], dn_all.at[x, t, rows_n]), (dyd_ref.at[rows_d, cols], dd_all.at[x, t, rows_d])
+
+    def a2a_own(src):
+        for k, (s, d) in enumerate(a2a_pieces(src, 0, col)):
+            pltpu.make_async_copy(s, d, a2a_recv.at[0, k]).start()
+
+    def a2a_send(src, first, last):
+        @pl.loop(first, last)
+        def _(t):
+            peer = (col + shift_of(t)) % NCOL
+            for k, (s, d) in enumerate(a2a_pieces(src, t, peer)):
+                pltpu.make_async_remote_copy(src_ref=s, dst_ref=d, send_sem=a2a_sent.at[k], recv_sem=a2a_recv.at[t // CHUNK, k],
+                                             device_id=(peer, row), device_id_type=MESH).start()
+
+    def by_core(go, *args):
+        pl.when(core == 0)(lambda: go(dyg_ref, *args))
+        pl.when(core == 1)(lambda: go(dyu_ref, *args))
+
+    def x_of(dx):
+        return (x + dx + NX) % NX
+
+    own, prev, succ, far = x, x_of(-1), x_of(1), x_of(2)
+    partner = x * 2 + 1 - core
+    to_succ, to_prev = succ * 2 + core, prev * 2 + core
+    routes = ((own, to_succ, 0, 2), (own, to_prev, 0, 2), (own, partner, 0, 2), (prev, to_succ, 0, 1), (prev, partner, 0, 2),
+              (succ, to_prev, 1, 1), (succ, partner, 0, 2), (far, partner, 0, 1), (far, partner, 1, 1))
+
+    def hop(k, ch):
+        slot, target, first, count = routes[k]
+        cols = pl.ds(ch * CHUNK + first * (CHUNK // 2), count * (CHUNK // 2))
+        refs = (dn_all.at[slot, cols, rows_n], dd_all.at[slot, cols, rows_d])
+        return [pltpu.make_async_remote_copy(
+            src_ref=ref, dst_ref=ref, send_sem=x_send.at[k, ch, p], recv_sem=x_recv.at[k, ch, p],
+            device_id=(col, target), device_id_type=MESH) for p, ref in enumerate(refs)]
+
+    def hop_start(ch, *ks):
+        for k in ks:
+            for copy in hop(k, ch):
+                copy.start()
+
+    def hop_wait(ch, *ks):
+        for k in ks:
+            for copy in hop(k, ch):
+                copy.wait_recv()
+
+    def x_first(ch):
+        cols = pl.ds(ch * CHUNK, CHUNK)
+        for k, ref in enumerate((dn_all.at[x, cols, rows_n], dd_all.at[x, cols, rows_d])):
+            pltpu.make_async_copy(ref, ref, a2a_recv.at[ch, k]).wait()
+        if DO_X:
+            hop_start(ch, 0, 1, 2)
+
+    def x_second(ch):
+        if DO_X:
+            hop_wait(ch, 0)
+            hop_start(ch, 3, 4)
+            hop_wait(ch, 1)
+            hop_start(ch, 5, 6)
+
+    def x_third(ch):
+        if DO_X:
+            hop_wait(ch, 3)
+            hop_start(ch, 7)
+            hop_wait(ch, 5)
+            hop_start(ch, 8)
+
+    def x_last(ch):
+        if DO_X:
+            hop_wait(ch, 2, 4, 6, 7, 8)
+
+    n_chunks = NCOL // CHUNK
+    events = {}
+    for ch in range(n_chunks):
+        for stage, at in zip((x_first, x_second, x_third), X_AT[ch]):
+            events.setdefault(at, []).append((stage, ch))
+
     if DO_W:
         for copy in fetch_own:
             copy.start()
+    if DO_A2A:
+        by_core(a2a_own)
+    if DO_W:
         for copy in fetch_own:
             copy.wait()
-        w_rings.start(0)
-
-    rows_n, rows_d = pl.ds(core * ng, ng), pl.ds(core * hd, hd)
-
-    def a2a(src):
-        @pl.loop(0, NCOL)
-        def _(shift):
-            peer = (col + shift) % NCOL
-            cols = pl.ds(pl.multiple_of(peer * tokens + x * quarter, quarter), quarter)
-            pieces = ((src.at[:, cols], dn_all.at[x, col, rows_n]), (dyd_ref.at[rows_d, cols], dd_all.at[x, col, rows_d]))
-
-            @pl.when(shift == 0)
-            def _():
-                for k, (s, d) in enumerate(pieces):
-                    pltpu.make_async_copy(s, d, a2a_sems.at[1, k]).start()
-
-            @pl.when(shift > 0)
-            def _():
-                for k, (s, d) in enumerate(pieces):
-                    pltpu.make_async_remote_copy(src_ref=s, dst_ref=d, send_sem=a2a_sems.at[0, k], recv_sem=a2a_sems.at[1, k],
-                                                 device_id=(peer, row), device_id_type=MESH).start()
-
-    if DO_A2A:
-        pl.when(core == 0)(lambda: a2a(dyg_ref))
-        pl.when(core == 1)(lambda: a2a(dyu_ref))
-
-    def x_of(dx):
-        return (x + dx + NX) % NX
-
-    half = NCOL // 2
-    every, low, high = pl.ds(0, NCOL), pl.ds(0, half), pl.ds(half, half)
-    own, prev, succ, far = x, x_of(-1), x_of(1), x_of(2)
-    partner = x * 2 + 1 - core
-
-    class Hop:
-        def __init__(self, k, slot, target, cols=every):
-            refs = (dn_all.at[slot, cols, rows_n], dd_all.at[slot, cols, rows_d])
-            self.copies = [pltpu.make_async_remote_copy(
-                src_ref=ref, dst_ref=ref, send_sem=x_send.at[k, p], recv_sem=x_recv.at[k, p],
-                device_id=(col, target), device_id_type=MESH) for p, ref in enumerate(refs)]
-
-        def start(self):
-            for copy in self.copies:
-                copy.start()
-
-        def wait_recv(self):
-            for copy in self.copies:
-                copy.wait_recv()
-
-        def wait_send(self):
-            for copy in self.copies:
-                copy.wait_send()
-
-    to_succ, to_prev = succ * 2 + core, prev * 2 + core
-    hops = [
-        Hop(0, own, to_succ), Hop(1, own, to_prev), Hop(2, own, partner),
-        Hop(3, prev, to_succ, low), Hop(4, prev, partner),
-        Hop(5, succ, to_prev, high), Hop(6, succ, partner),
-        Hop(7, far, partner, low), Hop(8, far, partner, high)]
-
-    def w_steps(first, last):
+    for r in range(ROUNDS + 1):
         if DO_W:
-            @pl.loop(first, last)
-            def _(step):
-                w_rings.forward(step)
-
-    w_steps(1, W_A)
-    if DO_A2A:
-        for k, ref in enumerate((dn_all.at[x, every, rows_n], dd_all.at[x, every, rows_d])):
-            pltpu.make_async_copy(ref, ref, a2a_sems.at[1, k]).wait()
-    if DO_X:
-        for k in (0, 1, 2):
-            hops[k].start()
-    w_steps(W_A, W_B)
-    if DO_X:
-        hops[0].wait_recv()
-        hops[3].start()
-        hops[4].start()
-        hops[1].wait_recv()
-        hops[5].start()
-        hops[6].start()
-    w_steps(W_B, LONG)
-    if DO_W:
-        w_rings.wait_recv(LONG - 1)
-    if DO_X:
-        hops[3].wait_recv()
-        hops[7].start()
-        hops[5].wait_recv()
-        hops[8].start()
-        for k in (2, 4, 6, 7, 8):
-            hops[k].wait_recv()
+            trees.round(r)
+        if DO_A2A:
+            first, last = max(1, A2A_AT[r]), A2A_AT[r + 1]
+            if first < last:
+                by_core(a2a_send, first, last)
+            for stage, ch in events.get(r, ()):
+                stage(ch)
 
     group = 4
-    if DO_MM:
-        @pl.loop(0, NCOL // group)
-        def _(g):
-            js = pl.ds(g * group, group)
-            lhs_n = jnp.concatenate([dn_all[q, js].reshape(group * nn, quarter) for q in range(NX)], axis=1)
-            lhs_d = jnp.concatenate([dd_all[q, js].reshape(group * nd, quarter) for q in range(NX)], axis=1)
-            dims = (((0,), (0,)), ((), ()))
-            part_n = lax.dot_general(lhs_n, wn_all[js].reshape(group * nn, wn_all.shape[2]), dims, preferred_element_type=F32)
-            part_a = lax.dot_general(lhs_d, wa_all[js].reshape(group * nd, wa_all.shape[2]), dims, preferred_element_type=F32)
-
-            @pl.when(g == 0)
-            def _():
-                acc_n[...] = part_n
-                acc_a[...] = part_a
-
-            @pl.when(g > 0)
-            def _():
-                acc_n[...] += part_n
-                acc_a[...] += part_a
-
-    own_n[...] = acc_n[...].astype(BF16)
-    own_a[...] = acc_a[...].astype(BF16)
+    for ch in range(n_chunks):
+        if DO_A2A:
+            for stage, late in events.get(ROUNDS + 1 + ch, ()):
+                stage(late)
+            x_last(ch)
+        if DO_MM:
+            @pl.loop(ch * (CHUNK // group), (ch + 1) * (CHUNK // group))
+            def _(g):
+                slots = pl.ds(g * group, group)
+                js = [(col - shift_of(g * group + i) + NCOL) % NCOL for i in range(group)]
+                lhs_n = jnp.concatenate([dn_all[q, slots].reshape(group * nn, quarter) for q in range(NX)], axis=1)
+                lhs_d = jnp.concatenate([dd_all[q, slots].reshape(group * nd, quarter) for q in range(NX)], axis=1)
+                dims = (((0,), (0,)), ((), ()))
+                part_n = lax.dot_general(lhs_n, jnp.concatenate([wn_all[j] for j in js], axis=0), dims, preferred_element_type=F32)
+                part_a = lax.dot_general(lhs_d, jnp.concatenate([wa_all[j] for j in js], axis=0), dims, preferred_element_type=F32)
+
+                @pl.when(g == 0)
+                def _():
+                    acc_n[...] = part_n
+                    acc_a[...] = part_a
+
+                @pl.when(g > 0)
+                def _():
+                    acc_n[...] += part_n
+                    acc_a[...] += part_a
+
     mine = pl.ds(pl.multiple_of(col * tokens, tokens), tokens)
-    place_own = [pltpu.make_async_copy(own_n, dxn_ref.at[mine], local_sem.at[0]),
-                 pltpu.make_async_copy(own_a, dxa_ref.at[mine], local_sem.at[1])]
-    for copy in place_own:
-        copy.start()
-    for copy in place_own:
-        copy.wait()
+    dxn_ref[mine, :] = acc_n[...].astype(BF16)
+    dxa_ref[mine, :] = acc_a[...].astype(BF16)
 
     def span(ref, offset, count):
         def part(cycle, origin):
@@ -257,13 +315,13 @@
         grad_n[...] += jnp.dot(dyn_buf[slot], xn_buf[slot], preferred_element_type=F32)
         grad_d[...] += jnp.dot(dyd_buf[slot], xa_buf[slot], preferred_element_type=F32)
 
-    if DO_AG:
-        ag.start(0)
-    grad_n[...] = jnp.zeros_like(grad_n)
-    grad_d[...] = jnp.zeros_like(grad_d)
     if DO_DW:
         for copy in tile_copies(0, 0):
             copy.start()
+    grad_n[...] = jnp.zeros_like(grad_n)
+    grad_d[...] = jnp.zeros_like(grad_d)
+    if DO_AG:
+        ag.start(0)
     per_step = n_tiles // DW_STEPS
 
     @pl.loop(1, DW_STEPS + 1)
@@ -394,13 +452,18 @@
         ag.wait_recv(LONG - 1)
 
     if DO_X:
-        for hop in hops:
-            hop.wait_send()
+        for ch in range(n_chunks):
+            for k in range(len(routes)):
+                for copy in hop(k, ch):
+                    copy.wait_send()
     if DO_A2A:
         for k, ref in enumerate((dn_all.at[0, pl.ds(0, NCOL - 1), pl.ds(0, ng)], dd_all.at[0, pl.ds(0, NCOL - 1), pl.ds(0, hd)])):
-            pltpu.make_async_copy(ref, ref, a2a_sems.at[0, k]).wait()
+            pltpu.make_async_copy(ref, ref, a2a_sent.at[k]).wait()
     if DO_W:
-        w_rings.wait_sends([lambda n: wn_all.at[pl.ds(0, n), pl.ds(0, ng)], lambda n: wa_all.at[pl.ds(0, n), pl.ds(0, hd)]])
+        for tree, cuts in enumerate(w_cuts):
+            for k, (ref, _, count) in enumerate(cuts):
+                ref = ref.at[pl.ds(0, NCOL - 1), pl.ds(0, count)]
+                pltpu.make_async_copy(ref, ref, w_send.at[tree, k]).wait()
     if DO_AG:
         ag.wait_sends([lambda n, ref=ref, size=size: ref.at[pl.ds(0, n * size)] for ref, size in sizes])
     if DO_ST:
@@ -409,8 +472,51 @@
 
 
 DO_W = DO_A2A = DO_X = DO_MM = DO_AG = DO_DW = DO_ST = True
-W_A, W_B, DW_STEPS = 6, 11, 8
+CHUNK, DW_STEPS = 8, 8
+ROUNDS = NY // 2 + NZ // 2
+A2A_AT = (0, 8, 16, 24, 32, 32, 32, 32)
+X_AT = ((1, 2, 3), (2, 3, 4), (3, 4, 5), (4, 5, 7))
+W_CUT = 128
 TILE = 512
+
+
+VMEM_LIMIT = 33 * 1024 * 1024
+PIECES = 8
+
+
+def finish_kernel(wg_ref, wu_ref, wd_ref, r_ref, c_ref, dxn_ref, dxa_ref,
+                  wg_out, wu_out, wd_out, rg_out, cg_out, ru_out, cu_out, rd_out, cd_out, dxn_out, dxa_out, sems):
+    rows = dxn_ref.shape[0] // PIECES
+    copies = [pltpu.make_async_copy(src.at[pl.ds(k * rows, rows)], dst.at[pl.ds(k * rows, rows)], sems.at[p, k])
+              for p, (src, dst) in enumerate(((dxa_ref, dxa_out), (dxn_ref, dxn_out))) for k in range(PIECES)]
+    for copy in copies:
+        copy.start()
+    for src, dst in ((wg_ref, wg_out), (wu_ref, wu_out), (wd_ref, wd_out)):
+        dst[...] = src[...]
+    for src, outs in ((r_ref, (rg_out, ru_out, rd_out)), (c_ref, (cg_out, cu_out, cd_out))):
+        at = 0
+        for out in outs:
+            out[...] = src[:, at:at + out.shape[1]]
+            at += out.shape[1]
+    for copy in copies:
+        copy.wait()
+
+
+def finish(wg, wu, wd, r_all, c_all, dxn, dxa):
+    vmem, hbm = pl.BlockSpec(memory_space=pltpu.VMEM), pl.BlockSpec(memory_space=pl.ANY)
+    shape = jax.ShapeDtypeStruct
+    ng, m = wg.shape
+    nd, ma = wd.shape
+    stats = [shape((1, n), F32) for n in (m, ng, m, ng, ma, nd)]
+    return pl.pallas_call(
+        finish_kernel,
+        out_shape=[shape(w.shape, F32) for w in (wg, wu, wd)] + stats + [shape(dxn.shape, BF16), shape(dxa.shape, BF16)],
+        in_specs=[vmem] * 7,
+        out_specs=[vmem] * 9 + [hbm] * 2,
+        scratch_shapes=[pltpu.SemaphoreType.DMA((2, PIECES))],
+        compiler_params=pltpu.CompilerParams(vmem_limit_bytes=1 * 1024 * 1024),
+        name='finish',
+    )(wg, wu, wd, r_all, c_all, dxn, dxa)
 
 
 def fused_step(dyg, dyu, dyd, xn, xa, wn, wa, wg, wu, wd, r_all, c_all, hyper):
@@ -424,9 +530,9 @@
     return pl.pallas_call(
         step_kernel,
         out_shape=(shape(wg.shape, F32), shape(wu.shape, F32), shape(wd.shape, F32), shape(r_all.shape, F32), shape(c_all.shape, F32),
-                   shape(xn.shape, BF16), shape(xa.shape, BF16)),
+                   pltpu.VMEM(xn.shape, BF16), pltpu.VMEM(xa.shape, BF16)),
         in_specs=[hbm] * 5 + [vmem] * 7 + [smem],
-        out_specs=(vmem,) * 5 + (hbm,) * 2,
+        out_specs=(vmem,) * 7,
         scratch_shapes=[
             pltpu.VMEM((NX, NCOL, nn, tokens // NX), BF16),
             pltpu.VMEM((NX, NCOL, nd, tokens // NX), BF16),
@@ -434,8 +540,6 @@
             pltpu.VMEM((NCOL, nd, ma), BF16),
             pltpu.VMEM((tokens, m), F32),
             pltpu.VMEM((tokens, ma), F32),
-            pltpu.VMEM((tokens, m), BF16),
-            pltpu.VMEM((tokens, ma), BF16),
             pltpu.VMEM((2, TILE, m), BF16),
             pltpu.VMEM((2, TILE, ma), BF16),
             pltpu.VMEM((2, nn, TILE), BF16),
@@ -447,10 +551,11 @@
             pltpu.VMEM((NROW, 1, 128), F32),
             pltpu.VMEM((NROW, 1, 128), F32),
             pltpu.VMEM((NCOL, 1, 128), F32),
-            dma((4, 2)), dma((4, LONG, 2)), dma((4, 3)), dma((4, LONG, 3)), dma((2,)), dma((2, 2)), dma((9, 2)), dma((9, 2)),
+            dma((2, 2)), dma((2, NY, NZ, 2)), dma((4, 3)), dma((4, LONG, 3)), dma((2,)), dma((2,)), dma((NCOL // CHUNK, 2)),
+            dma((9, NCOL // CHUNK, 2)), dma((9, NCOL // CHUNK, 2)),
             dma((2, 5)), dma((5,)), dma((5,)),
         ],
-        compiler_params=pltpu.CompilerParams(has_side_effects=True, vmem_limit_bytes=60 * 1024 * 1024),
+        compiler_params=pltpu.CompilerParams(has_side_effects=True, vmem_limit_bytes=VMEM_LIMIT),
         name='fused_step',
     )(dyg, dyu, dyd, xn, xa, wn, wa, wg, wu, wd, r_all, c_all, hyper)
 
@@ -469,10 +574,8 @@
         wa = wd.astype(BF16)
         r_all = jnp.concatenate([r_gate, r_up, r_down])[None]
         c_all = jnp.concatenate([c_gate, c_up, c_down])[None]
-        wg, wu, wd, r_all, c_all, dx_norm, dx_act = fused_step(
-            dy_gate.T, dy_up.T, dy_down.T, x_norm, x_act, wn, wa, wg, wu, wd, r_all, c_all, hyper_params)
-        r_all, c_all = r_all[0], c_all[0]
-        return (wg.T, wu.T, wd.T, r_all[:m], c_all[:ng], r_all[m:2 * m], c_all[ng:2 * ng], r_all[2 * m:], c_all[2 * ng:],
-                dx_norm, dx_act)
+        out = fused_step(dy_gate.T, dy_up.T, dy_down.T, x_norm, x_act, wn, wa, wg, wu, wd, r_all, c_all, hyper_params)
+        wg, wu, wd, rg, cg, ru, cu, rd, cd, dx_norm, dx_act = finish(*out)
+        return (wg.T, wu.T, wd.T, rg[0], cg[0], ru[0], cu[0], rd[0], cd[0], dx_norm, dx_act)
 
     return jax.shard_map(body, mesh=mesh, in_specs=in_specs, out_specs=out_specs, check_vma=False)

time: 348 us -> 308 us (0.89)
  local copies, waits for them, and re-layouts: 35.3 us -> 5.25 us
  Pallas kernels: 306 us -> 295 us
    unnamed x5 -> x10, local copies, waits for them, and re-layouts: 29 us -> 4.09 us
    pallas_call x1, Pallas kernels: 306 us -> 285 us  [fused_step(): pl.pallas_call(step_kernel, out_shape=(shape(wg.shape, F32), shape(wu.sha...]
    pallas_call x0 -> x1, Pallas kernels: none -> 10.6 us  [finish(): pl.pallas_call(finish_kernel, out_shape=[shape(w.shape, F32) for w in (wg...]
    slice x4 -> x0, local copies, waits for them, and re-layouts: 5.12 us -> none  [the longest x1 1.34 us: body(): c_all[ng:2 * ng]]
where the time goes in v3:
time: 308 us; the launch traced here: 307 us
  Pallas kernels  295 us (96%)
  other arithmetic  5.36 us (2%)
  local copies, waits for them, and re-layouts  5.25 us (2%)
    pallas_call x1, Pallas kernels, fused_step(): pl.pallas_call(step_kernel, out_shape=(shape(wg.shape, F32), shape(wu.sha...  285 us
    pallas_call x1, Pallas kernels, finish(): pl.pallas_call(finish_kernel, out_shape=[shape(w.shape, F32) for w in (wg...  10.6 us

profile of v3, /device:TPU:1, one launch (start us, length us, event | category | flops | bytes accessed | tf_op | source)
XLA Modules:
  0.0 306.7 jit_solution(11952429993414730424)
XLA Ops:
  0.6 0.8 pad_maximum_fusion.2
  1.4 0.6 broadcast_in_dim.7.c_ref
  2.0 0.7 pad_maximum_fusion.1
  2.7 0.6 broadcast_in_dim.6.r_ref
  3.3 1.6 bitcast_convert_fusion.wa_ref
  4.9 1.0 bitcast_convert_fusion.1
  5.9 0.7 pad_maximum_fusion.wn_ref
  6.6 284.9 %fused_step.1 = (f32[160,256]{1,0:T(8,128)}, f32[160,256]{1,0:T(8,128)}, f32[64,640]{1,0:T(8,128)}, f32[1,1152]{1,0:T(1,128)}, f32[1,384]{1,0:T(1,128)}, /*index...) custom-call(bf16[160,16384]{1,0:T(8,128)(2,1)} %bitcast.17, bf16[160,16384]{1,0:T(8,128)(2,1)} %bitcast.18, ...), custom_call_target="tpu_custom_call" | custom-call | tf_op jit(solution)/shard_map/fused_step/pallas_call | solution.py:530
  291.4 0.0 copy-start
  291.4 0.9 copy-done
  292.3 0.0 copy-start.1
  292.4 0.9 copy-done.1
  293.3 0.0 copy-start.2
  293.3 0.9 copy-done.2
  294.2 0.0 copy-start.3
  294.2 0.7 copy-done.3
  294.9 0.0 copy-start.4
  294.9 0.7 copy-done.4
  295.5 10.6 %finish.1 = (f32[160,256]{1,0:T(8,128)}, f32[160,256]{1,0:T(8,128)}, f32[64,640]{1,0:T(8,128)}, f32[1,256]{1,0:T(1,128)}, f32[1,160]{1,0:T(1,128)}, /*index=5*/f...) custom-call(f32[160,256]{1,0:T(8,128)S(1)} %copy-done, ...), custom_call_target="tpu_custom_call" | custom-call | tf_op jit(solution)/shard_map/finish/pallas_call | solution.py:511
  306.1 0.6 reduce
Async XLA Ops:
  291.4 0.9 copy-start
  292.3 0.9 copy-start.1
  293.3 0.9 copy-start.2
  294.2 0.7 copy-start.3
  294.9 0.7 copy-start.4

commit v4 on v3

--- a/solution.py
+++ b/solution.py
@@ -129,12 +129,13 @@
                             self.copy(tree, k, (ey, ez), target).start()
 
 
-def step_kernel(dyg_ref, dyu_ref, dyd_ref, xn_ref, xa_ref, wn_ref, wa_ref, wg_ref, wu_ref, wd_ref, r_ref, c_ref, hyper_ref,
+def step_kernel(dyg_ref, dyu_ref, dyd_ref, xn_ref, xa_ref, wg_ref, wu_ref, wd_ref,
+                rg_ref, cg_ref, ru_ref, cu_ref, rd_ref, cd_ref, hyper_ref,
                 wg_out, wu_out, wd_out, r_out, c_out, dxn_ref, dxa_ref,
                 dn_all, dd_all, wn_all, wa_all, acc_n, acc_a,
                 xn_buf, xa_buf, dyn_buf, dyd_buf, grad_n, grad_d,
                 col_msg, row_msg, u_msg, r_msg, z_msg,
-                w_send, w_recv, ag_send, ag_recv, local_sem, a2a_sent, a2a_recv, x_send, x_recv, tile_sems, st_send, st_recv):
+                w_send, w_recv, ag_send, ag_recv, a2a_sent, a2a_recv, x_send, x_recv, tile_sems, st_send, st_recv):
     col, row = lax.axis_index('col'), lax.axis_index('row')
     x, core = row // 2, row % 2
     tokens = dxn_ref.shape[0] // NCOL
@@ -143,8 +144,9 @@
     nd = dyd_ref.shape[0]
     nn = 2 * ng
     hd = nd // 2
-    fetch_own = [pltpu.make_async_copy(wn_ref, wn_all.at[col], local_sem.at[0]),
-                 pltpu.make_async_copy(wa_ref, wa_all.at[col], local_sem.at[1])]
+    wn_all[col, pl.ds(0, ng), :] = wg_ref[...].astype(BF16)
+    wn_all[col, pl.ds(ng, ng), :] = wu_ref[...].astype(BF16)
+    wa_all[col] = wd_ref[...].astype(BF16)
 
     def w_piece(ref, first, count):
         return lambda origin: ref.at[origin, pl.ds(first, count)]
@@ -235,14 +237,10 @@
         for stage, at in zip((x_first, x_second, x_third), X_AT[ch]):
             events.setdefault(at, []).append((stage, ch))
 
-    if DO_W:
-        for copy in fetch_own:
-            copy.start()
     if DO_A2A:
         by_core(a2a_own)
-    if DO_W:
-        for copy in fetch_own:
-            copy.wait()
+    grad_n[...] = jnp.zeros_like(grad_n)
+    grad_d[...] = jnp.zeros_like(grad_d)
     for r in range(ROUNDS + 1):
         if DO_W:
             trees.round(r)
@@ -318,8 +316,6 @@
     if DO_DW:
         for copy in tile_copies(0, 0):
             copy.start()
-    grad_n[...] = jnp.zeros_like(grad_n)
-    grad_d[...] = jnp.zeros_like(grad_d)
     if DO_AG:
         ag.start(0)
     per_step = n_tiles // DW_STEPS
@@ -395,8 +391,10 @@
     n_r = r_total.shape[1] - 128
     lane_r = lax.broadcasted_iota(jnp.int32, (1, n_r), 1)
     lane_c = lax.broadcasted_iota(jnp.int32, (1, nn + nd), 1)
-    r_new = beta_two * r_ref[...] + (1.0 - beta_two) * (r_total[:, :n_r] / jnp.where(lane_r < 2 * m, n_cols, n_rows))
-    c_new = beta_two * c_ref[...] + (1.0 - beta_two) * (c_total / jnp.where(lane_c < nn, n_rows, n_cols))
+    r_old = jnp.concatenate([rg_ref[...], ru_ref[...], rd_ref[...]], axis=1)
+    c_old = jnp.concatenate([cg_ref[...], cu_ref[...], cd_ref[...]], axis=1)
+    r_new = beta_two * r_old + (1.0 - beta_two) * (r_total[:, :n_r] / jnp.where(lane_r < 2 * m, n_cols, n_rows))
+    c_new = beta_two * c_old + (1.0 - beta_two) * (c_total / jnp.where(lane_c < nn, n_rows, n_cols))
     r_out[...] = r_new
     c_out[...] = c_new
     r_cuts = ((0, m), (m, 2 * m), (2 * m, n_r))
@@ -474,8 +472,8 @@
 DO_W = DO_A2A = DO_X = DO_MM = DO_AG = DO_DW = DO_ST = True
 CHUNK, DW_STEPS = 8, 8
 ROUNDS = NY // 2 + NZ // 2
-A2A_AT = (0, 8, 16, 24, 32, 32, 32, 32)
-X_AT = ((1, 2, 3), (2, 3, 4), (3, 4, 5), (4, 5, 7))
+A2A_AT = (0, 16, 32, 32, 32, 32, 32, 32)
+X_AT = ((1, 2, 3), (1, 2, 3), (2, 3, 4), (2, 4, 5))
 W_CUT = 128
 TILE = 512
 
@@ -519,19 +517,19 @@
     )(wg, wu, wd, r_all, c_all, dxn, dxa)
 
 
-def fused_step(dyg, dyu, dyd, xn, xa, wn, wa, wg, wu, wd, r_all, c_all, hyper):
+def fused_step(dyg, dyu, dyd, xn, xa, wg, wu, wd, stats, hyper):
     tokens = xn.shape[0] // NCOL
     ng, nd, m, ma = dyg.shape[0], dyd.shape[0], xn.shape[1], xa.shape[1]
     nn = 2 * ng
     vmem, hbm = pl.BlockSpec(memory_space=pltpu.VMEM), pl.BlockSpec(memory_space=pl.ANY)
     smem = pl.BlockSpec(memory_space=pltpu.SMEM)
     dma = pltpu.SemaphoreType.DMA
-    shape = jax.ShapeDtypeStruct
     return pl.pallas_call(
         step_kernel,
-        out_shape=(shape(wg.shape, F32), shape(wu.shape, F32), shape(wd.shape, F32), shape(r_all.shape, F32), shape(c_all.shape, F32),
+        out_shape=(pltpu.VMEM(wg.shape, F32), pltpu.VMEM(wu.shape, F32), pltpu.VMEM(wd.shape, F32),
+                   pltpu.VMEM((1, 2 * m + ma), F32), pltpu.VMEM((1, nn + nd), F32),
                    pltpu.VMEM(xn.shape, BF16), pltpu.VMEM(xa.shape, BF16)),
-        in_specs=[hbm] * 5 + [vmem] * 7 + [smem],
+        in_specs=[hbm] * 5 + [vmem] * 9 + [smem],
         out_specs=(vmem,) * 7,
         scratch_shapes=[
             pltpu.VMEM((NX, NCOL, nn, tokens // NX), BF16),
@@ -551,13 +549,13 @@
             pltpu.VMEM((NROW, 1, 128), F32),
             pltpu.VMEM((NROW, 1, 128), F32),
             pltpu.VMEM((NCOL, 1, 128), F32),
-            dma((2, 2)), dma((2, NY, NZ, 2)), dma((4, 3)), dma((4, LONG, 3)), dma((2,)), dma((2,)), dma((NCOL // CHUNK, 2)),
+            dma((2, 2)), dma((2, NY, NZ, 2)), dma((4, 3)), dma((4, LONG, 3)), dma((2,)), dma((NCOL // CHUNK, 2)),
             dma((9, NCOL // CHUNK, 2)), dma((9, NCOL // CHUNK, 2)),
             dma((2, 5)), dma((5,)), dma((5,)),
         ],
         compiler_params=pltpu.CompilerParams(has_side_effects=True, vmem_limit_bytes=VMEM_LIMIT),
         name='fused_step',
-    )(dyg, dyu, dyd, xn, xa, wn, wa, wg, wu, wd, r_all, c_all, hyper)
+    )(dyg, dyu, dyd, xn, xa, wg, wu, wd, *stats, hyper)
 
 
 def solution(mesh):
@@ -568,13 +566,8 @@
     out_specs = (weight_spec,) * 3 + (P('row'), P('col')) * 3 + (act_spec, act_spec)
 
     def body(w_gate, w_up, w_down, x_norm, x_act, dy_gate, dy_up, dy_down, r_gate, c_gate, r_up, c_up, r_down, c_down, hyper_params):
-        m, ng = w_gate.shape
-        wg, wu, wd = w_gate.T, w_up.T, w_down.T
-        wn = jnp.concatenate([wg.astype(BF16), wu.astype(BF16)], axis=0)
-        wa = wd.astype(BF16)
-        r_all = jnp.concatenate([r_gate, r_up, r_down])[None]
-        c_all = jnp.concatenate([c_gate, c_up, c_down])[None]
-        out = fused_step(dy_gate.T, dy_up.T, dy_down.T, x_norm, x_act, wn, wa, wg, wu, wd, r_all, c_all, hyper_params)
+        stats = [v[None] for v in (r_gate, c_gate, r_up, c_up, r_down, c_down)]
+        out = fused_step(dy_gate.T, dy_up.T, dy_down.T, x_norm, x_act, w_gate.T, w_up.T, w_down.T, stats, hyper_params)
         wg, wu, wd, rg, cg, ru, cu, rd, cd, dx_norm, dx_act = finish(*out)
         return (wg.T, wu.T, wd.T, rg[0], cg[0], ru[0], cu[0], rd[0], cd[0], dx_norm, dx_act)
 

time: 308 us -> 283 us (0.919)
  Pallas kernels: 295 us -> 279 us
  other arithmetic: 5.36 us -> 0.61 us
  local copies, waits for them, and re-layouts: 5.25 us -> 1.27 us
    pallas_call x1, Pallas kernels: 285 us -> 268 us  [fused_step(): pl.pallas_call(step_kernel, out_shape=(pltpu.VMEM(wg.shape, F32), pltpu.V...]
    unnamed x10 -> x0, local copies, waits for them, and re-layouts: 4.09 us -> none
where the time goes in v4:
time: 283 us; the launch traced here: 281 us
  Pallas kernels  279 us (99%)
    pallas_call x1, Pallas kernels, fused_step(): pl.pallas_call(step_kernel, out_shape=(pltpu.VMEM(wg.shape, F32), pltpu.V...  268 us
    pallas_call x1, Pallas kernels, finish(): pl.pallas_call(finish_kernel, out_shape=[shape(w.shape, F32) for w in (wg...  10.6 us

profile of v4, /device:TPU:1, one launch (start us, length us, event | category | flops | bytes accessed | tf_op | source)
XLA Modules:
  0.0 281.0 jit_solution(15187515727987518520)
XLA Ops:
  0.6 1.3 broadcast_in_dim.22.rd_ref
  1.9 267.9 %fused_step.1 = (f32[160,256]{1,0:T(8,128)S(1)}, f32[160,256]{1,0:T(8,128)S(1)}, f32[64,640]{1,0:T(8,128)S(1)}, f32[1,1152]{1,0:T(1,128)S(1)}, f32[1,384]{1,0:T(...) custom-call(bf16[160,16384]{1,0:T(8,128)(2,1)} %bitcast.19, bf16[160,16384]{1,0:T(8,128)(2,1)} %bitcast.20, ...), custom_call_target="tpu_custom_call" | custom-call | tf_op jit(solution)/shard_map/fused_step/pallas_call | solution.py:527
  269.9 10.6 %finish.1 = (f32[160,256]{1,0:T(8,128)}, f32[160,256]{1,0:T(8,128)}, f32[64,640]{1,0:T(8,128)}, f32[1,256]{1,0:T(1,128)}, f32[1,160]{1,0:T(1,128)}, /*index=5*/f...) custom-call(f32[160,256]{1,0:T(8,128)S(1)} %get-tuple-element.29.wg_, ...), custom_call_target="tpu_custom_call" | custom-call | tf_op jit(solution)/shard_map/finish/pallas_call | solution.py:509
  280.4 0.6 reduce
